TPU v7x, 16 devices: a whole 2x2x2 slice. The times are simulated.
16 devices in a mesh: dp: 16 (over z, y, x, core).
Axes of the slice: x: 2, y: 2, z: 2, core: 2. Of those that a mesh axis runs over, the one named last changes fastest.
Arguments:
- x_in: bfloat16 [32768, 1024], P('dp')
- dy_mid: bfloat16 [32768, 4096], P('dp')
- x_mid: bfloat16 [32768, 4096], P('dp')
- dy_out: bfloat16 [32768, 1024], P('dp')
- w_fc1: float32 [1024, 4096], replicated
- w_fc2: float32 [4096, 1024], replicated
- stat_left: float32 [32, 512, 512], P('dp')
- stat_right: float32 [32, 512, 512], P('dp')
- root_left: float32 [32, 512, 512], P('dp')
- root_right: float32 [32, 512, 512], P('dp')
- graft_sq: float32 [32, 512, 512], P('dp')
- momentum: float32 [32, 512, 512], P('dp')
Outputs:
- output 1: float32 [1024, 4096], replicated
- output 2: float32 [4096, 1024], replicated
- output 3: float32 [32, 512, 512], P('dp')
- output 4: float32 [32, 512, 512], P('dp')
- output 5: float32 [32, 512, 512], P('dp')
- output 6: float32 [32, 512, 512], P('dp')
All inputs are finite; a program needn't handle non-finite values.
Results may differ from a plain program's by a relative error of at most 0.001.
Values are sent between devices in bfloat16 or wider.
A program may use at most 1 GiB of HBM per device.

v0:
```python
import jax
import jax.numpy as jnp
from jax import lax
from jax.sharding import PartitionSpec as P

STEP = 10
STAT_DECAY = 0.999
MOM_DECAY = 0.9
GRAFT_EPS = 1e-8
LEARN_RATE = 0.01
WEIGHT_DECAY = 1e-4
BIAS_CORR = 1.0 - STAT_DECAY ** STEP


def grad_blocks(x_rows, dy_rows, block_dim):
    n_tok, n_in = x_rows.shape
    n_out = dy_rows.shape[1]
    in_blocks = -(-n_in // block_dim)
    out_blocks = -(-n_out // block_dim)
    x_pad = jnp.pad(x_rows, ((0, 0), (0, in_blocks * block_dim - n_in))).reshape(n_tok, in_blocks, block_dim)
    dy_pad = jnp.pad(dy_rows, ((0, 0), (0, out_blocks * block_dim - n_out))).reshape(n_tok, out_blocks, block_dim)
    grad_tiles = jnp.einsum('tri,tcj->rcij', x_pad, dy_pad, preferred_element_type=jnp.float32)
    return grad_tiles.reshape(in_blocks * out_blocks, block_dim, block_dim)


def from_blocks(dir_blocks, n_rows, n_cols):
    block_dim = dir_blocks.shape[-1]
    row_blocks = -(-n_rows // block_dim)
    col_blocks = -(-n_cols // block_dim)
    full_mat = dir_blocks.reshape(row_blocks, col_blocks, block_dim, block_dim).transpose(0, 2, 1, 3)
    return full_mat.reshape(row_blocks * block_dim, col_blocks * block_dim)[:n_rows, :n_cols]


def keep_mask(block_ids, n_model, n_hidden, block_dim):
    model_blocks = -(-n_model // block_dim)
    hidden_blocks = -(-n_hidden // block_dim)
    half_count = model_blocks * hidden_blocks
    is_first = block_ids < half_count
    local_ids = block_ids % half_count
    row_first = jnp.minimum(n_model - (local_ids // hidden_blocks) * block_dim, block_dim)
    col_first = jnp.minimum(n_hidden - (local_ids % hidden_blocks) * block_dim, block_dim)
    row_second = jnp.minimum(n_hidden - (local_ids // model_blocks) * block_dim, block_dim)
    col_second = jnp.minimum(n_model - (local_ids % model_blocks) * block_dim, block_dim)
    row_count = jnp.where(is_first, row_first, row_second)
    col_count = jnp.where(is_first, col_first, col_second)
    offsets = jnp.arange(block_dim)
    return (offsets[None, :, None] < row_count[:, None, None]) & (offsets[None, None, :] < col_count[:, None, None])


def stat_update(grad_blk, stat_left, stat_right):
    left_prod = jnp.einsum('nik,njk->nij', grad_blk, grad_blk, precision=lax.Precision.HIGHEST, preferred_element_type=jnp.float32)
    right_prod = jnp.einsum('nki,nkj->nij', grad_blk, grad_blk, precision=lax.Precision.HIGHEST, preferred_element_type=jnp.float32)
    return STAT_DECAY * stat_left + (1.0 - STAT_DECAY) * left_prod, STAT_DECAY * stat_right + (1.0 - STAT_DECAY) * right_prod


def direction_update(grad_blk, root_left, root_right, graft_sq, momentum, keep_tiles):
    left_mul = jnp.einsum('nij,njk->nik', root_left, grad_blk, precision=lax.Precision.HIGHEST, preferred_element_type=jnp.float32)
    precond = jnp.einsum('nij,njk->nik', left_mul, root_right, precision=lax.Precision.HIGHEST, preferred_element_type=jnp.float32)
    precond = jnp.where(keep_tiles, precond, 0.0)
    new_sq = STAT_DECAY * graft_sq + (1.0 - STAT_DECAY) * grad_blk * grad_blk
    graft_dir = grad_blk / (jnp.sqrt(new_sq / BIAS_CORR) + GRAFT_EPS)
    graft_norm = jnp.sqrt(jnp.sum(graft_dir * graft_dir, axis=(1, 2)))
    pre_norm = jnp.sqrt(jnp.sum(precond * precond, axis=(1, 2)))
    new_mom = MOM_DECAY * momentum + precond * (graft_norm / pre_norm)[:, None, None]
    return new_sq, new_mom


def apply_update(w_fc1, w_fc2, dir_blocks):
    n_model, n_hidden = w_fc1.shape
    half_count = dir_blocks.shape[0] // 2
    dir_fc1 = from_blocks(dir_blocks[:half_count], n_model, n_hidden)
    dir_fc2 = from_blocks(dir_blocks[half_count:], n_hidden, n_model)
    new_w1 = w_fc1 - LEARN_RATE * (dir_fc1.astype(jnp.float32) + WEIGHT_DECAY * w_fc1)
    new_w2 = w_fc2 - LEARN_RATE * (dir_fc2.astype(jnp.float32) + WEIGHT_DECAY * w_fc2)
    return new_w1, new_w2


def solution(mesh):
    n_dev = mesh.shape['dp']

    def per_device(x_in, dy_mid, x_mid, dy_out, w_fc1, w_fc2, stat_left, stat_right, root_left, root_right, graft_sq, momentum):
        block_dim = stat_left.shape[-1]
        n_model, n_hidden = w_fc1.shape
        own_count = stat_left.shape[0]
        local_grad = jnp.concatenate([grad_blocks(x_in, dy_mid, block_dim), grad_blocks(x_mid, dy_out, block_dim)], axis=0)
        own_grad = lax.psum_scatter(local_grad, 'dp', scatter_dimension=0, tiled=True) / n_dev
        block_ids = lax.axis_index('dp') * own_count + jnp.arange(own_count)
        keep_tiles = keep_mask(block_ids, n_model, n_hidden, block_dim)
        new_left, new_right = stat_update(own_grad, stat_left, stat_right)
        new_sq, new_mom = direction_update(own_grad, root_left, root_right, graft_sq, momentum, keep_tiles)
        all_dir = lax.all_gather(new_mom.astype(jnp.bfloat16), 'dp', axis=0, tiled=True)
        new_w1, new_w2 = apply_update(w_fc1, w_fc2, all_dir)
        return new_w1, new_w2, new_left, new_right, new_sq, new_mom

    row_spec = P('dp', None)
    rep_spec = P(None, None)
    tile_spec = P('dp', None, None)
    in_specs = (row_spec, row_spec, row_spec, row_spec, rep_spec, rep_spec, tile_spec, tile_spec, tile_spec, tile_spec, tile_spec, tile_spec)
    out_specs = (rep_spec, rep_spec, tile_spec, tile_spec, tile_spec, tile_spec)
    return jax.shard_map(per_device, mesh=mesh, in_specs=in_specs, out_specs=out_specs, check_vma=False)
```

profile of v0, /device:TPU:0, one launch (start us, length us, event | category | flops | bytes accessed | tf_op | source)
XLA Modules:
  0.0 727.5 jit_solution(10101509305069753645)
XLA Ops:
  7.2 0.0 copy-start
  7.2 0.0 reduce-scatter.2.cloned.1.call-start
  7.2 22.6 %copy.50 = bf16[2048,4096]{0,1:T(8,128)(2,1)} copy(bf16[2048,4096]{1,0:T(8,128)(2,1)} %param.13) | data formatting | bytes 33554432 | tf_op jit(solution)/shard_map/reshape | solution.py:21
  29.8 23.5 %convolution_bitcast_fusion = f32[2,8,512,512]{2,3,0,1:T(8,128)} fusion(bf16[2048,8,512,1]{0,2,3,1:T(8,128)(2,1)} %bitcast.63, bf16[256,2,8,512]{3,2,1,0:T(8,128)(2,1)} %bitcast.66), kind=kOutput, calls=%fused_computation.8 | convolution fusion | flops 17179869184 | bytes 37748736 | tf_op jit(solution)/shard_map/tri,tcj->rcij/dot_general | solution.py:22
  53.3 17.6 %copy.36 = f32[2,8,512,512]{3,2,1,0:T(8,128)} copy(f32[2,8,512,512]{2,3,0,1:T(8,128)} %convolution_bitcast_fusion) | data formatting | bytes 33554432 | tf_op jit(solution)/shard_map/tri,tcj->rcij/transpose | solution.py:22
  70.9 6.4 copy.51
  77.3 23.5 %fusion.2 = f32[8,2,512,512]{2,3,0,1:T(8,128)} fusion(bf16[2048,2,512,1]{0,2,3,1:T(8,128)(2,1)} %bitcast.64, bf16[256,8,8,512]{3,2,1,0:T(8,128)(2,1)} %bitcast.65), kind=kOutput, calls=%fused_computation.9 | convolution fusion | flops 17179869184 | bytes 37748736 | tf_op jit(solution)/shard_map/tri,tcj->rcij/dot_general | solution.py:22
  100.8 17.3 %copy.39 = f32[8,2,512,512]{3,2,1,0:T(8,128)} copy(f32[8,2,512,512]{2,3,0,1:T(8,128)} %fusion.2) | data formatting | bytes 33554432 | tf_op jit(solution)/shard_map/tri,tcj->rcij/transpose | solution.py:22
  118.1 24.1 %pad_maximum_fusion = f32[32,512,512]{2,1,0:T(8,128)} fusion(f32[16,512,512]{2,1,0:T(8,128)} %bitcast.60, f32[16,512,512]{2,1,0:T(8,128)} %bitcast.59), kind=kLoop, calls=%fused_computation | loop fusion | flops 8388608 | bytes 67108864 | tf_op jit(solution)/shard_map/concatenate | solution.py:85
  142.2 0.0 reduce-scatter.2.cloned.1.call-update
  142.2 0.2 all-gather.2.cloned.1.call-start
  142.5 0.1 iota_compare_fusion
  142.6 0.1 iota_compare_fusion.1
  142.6 348.4 %reduce-scatter.2.cloned.1.call-done = f32[2,512,512]{2,1,0:T(8,128)} async-done(((f32[32,512,512]{2,1,0:T(8,128)}), f32[2,512,512]{2,1,0:T(8,128)}) %reduce-scatter.2.cloned.1.call-update) | async-done | bytes 2097168 | tf_op jit(solution)/shard_map/reduce_scatter | solution.py:86
  491.0 5.7 fusion.6
  496.8 0.0 copy-start.4
  496.8 3.8 multiply_reduce_fusion
  500.7 2.5 multiply_reduce_fusion.1
  503.2 2.2 fusion.21
  505.4 0.0 all-gather.2.cloned.1.call-update
  505.5 6.4 multiply_add_fusion
  511.9 5.1 multiply_add_fusion.1
  517.0 62.8 %all-gather.2.cloned.1.call-done = bf16[32,512,512]{2,1,0:T(8,128)(2,1)} async-done(((bf16[2,512,512]{2,1,0:T(8,128)(2,1)}), bf16[32,512,512]{2,1,0:T(8,128)(2,1)}) %all-gather.2.cloned.1.call-update) | async-done | bytes 16777232 | tf_op jit(solution)/shard_map/all_gather | solution.py:91
  579.8 11.5 %fusion.22 = (bf16[16,512,512]{2,1,0:T(8,128)(2,1)}, bf16[16,512,512]{2,1,0:T(8,128)(2,1)}) fusion(bf16[32,512,512]{2,1,0:T(8,128)(2,1)} %all-gather.2.cloned.1.call-done), kind=kLoop, calls=%fused_computation.56 | loop fusion | bytes 33554432 | tf_op jit(solution)/shard_map/slice | solution.py:72
  591.3 11.8 %convert_bitcast_fusion = f32[8,512,2,512]{3,1,2,0:T(8,128)} fusion(bf16[8,2,512,512]{3,2,1,0:T(8,128)(2,1)} %bitcast.62), kind=kLoop, calls=%fused_computation.4 | loop fusion | flops 4194304 | bytes 25165824 | tf_op jit(solution)/shard_map/convert_element_type | solution.py:74
  603.2 27.7 %copy.43 = f32[8,512,2,512]{3,2,1,0:T(2,128)S(1)} copy(f32[8,512,2,512]{3,1,2,0:T(8,128)} %convert_bitcast_fusion) | data formatting | bytes 33554432 | tf_op jit(solution)/shard_map/convert_element_type | solution.py:74
  630.9 7.9 %copy.55 = f32[512,8,2,512]{3,1,2,0:T(8,128)} copy(f32[512,8,2,512]{3,2,1,0:T(2,128)S(1)} %bitcast.57) | data formatting | bytes 33554432
  638.8 11.8 %convert_bitcast_fusion.1 = f32[2,512,8,512]{3,1,2,0:T(8,128)} fusion(bf16[2,8,512,512]{3,2,1,0:T(8,128)(2,1)} %bitcast.61), kind=kLoop, calls=%fused_computation.5 | loop fusion | flops 4194304 | bytes 25165824 | tf_op jit(solution)/shard_map/convert_element_type | solution.py:73
  650.7 18.2 %copy.42 = f32[2,512,8,512]{3,2,1,0:T(8,128)} copy(f32[2,512,8,512]{3,1,2,0:T(8,128)} %convert_bitcast_fusion.1) | data formatting | bytes 33554432 | tf_op jit(solution)/shard_map/convert_element_type | solution.py:73
  668.8 21.3 %copy.54 = f32[128,8,8,512]{3,1,2,0:T(8,128)} copy(f32[128,8,8,512]{3,2,1,0:T(8,128)} %bitcast.58) | data formatting | bytes 33554432
  690.1 12.8 %multiply_subtract_fusion = f32[4096,1024]{1,0:T(8,128)} fusion(f32[4096,1024]{1,0:T(8,128)} %param.17, f32[4096,1024]{1,0:T(8,128)S(1)} %bitcast.55), kind=kLoop, calls=%fused_computation.6 | loop fusion | flops 16777216 | bytes 50331648 | tf_op jit(solution)/shard_map/sub | solution.py:74
  702.9 17.3 %multiply_subtract_fusion.1 = f32[1024,4096]{1,0:T(8,128)} fusion(f32[1024,4096]{1,0:T(8,128)} %param.16, f32[1024,4096]{1,0:T(8,128)} %bitcast.56), kind=kLoop, calls=%fused_computation.7 | loop fusion | flops 16777216 | bytes 50331648 | tf_op jit(solution)/shard_map/sub | solution.py:73
  (23 shorter events, 0.1 us)
Async XLA Ops:
  7.2 489.6 %copy-start = (f32[2,512,512]{2,1,0:T(8,128)S(1)}, f32[2,512,512]{2,1,0:T(8,128)}, u32[]{:S(2)}) copy-start(f32[2,512,512]{2,1,0:T(8,128)} %param.21) | copy-start | bytes 6291460
  7.2 483.9 %reduce-scatter.2.cloned.1.call-start = ((), (), s32[]{:S(2)}) async-start(), calls=%async_computation.1 | async-start | bytes 35651584 | tf_op jit(solution)/shard_map/reduce_scatter | solution.py:86
  142.2 437.6 %all-gather.2.cloned.1.call-start = ((), (), s32[]{:S(2)}) async-start(), calls=%async_computation.2 | async-start | bytes 17825792 | tf_op jit(solution)/shard_map/all_gather | solution.py:91
  496.8 3.9 copy-start.2
  496.8 3.9 copy-start.4
  500.7 2.5 copy-start.5
  503.2 2.2 copy-start.3
  505.4 6.5 copy-start.6
  650.7 39.4 %slice-start = ((s8[16777216]{0:T(1024)(128)(4,1)}), s8[4194304]{0:T(1024)(128)(4,1)S(1)}, s32[]{:S(2)}) async-start(s8[16777216]{0:T(1024)(128)(4,1)} %bitcast.53), calls=%async_computation.3 | async-start | bytes 8388608
  650.7 39.4 %slice-start.1 = ((s8[16777216]{0:T(1024)(128)(4,1)}), s8[4194304]{0:T(1024)(128)(4,1)S(1)}, s32[]{:S(2)}) async-start(s8[16777216]{0:T(1024)(128)(4,1)} %bitcast.53), calls=%async_computation.4 | async-start | bytes 8388608
  668.8 21.3 %slice-start.2 = ((s8[16777216]{0:T(1024)(128)(4,1)}), s8[4194304]{0:T(1024)(128)(4,1)S(1)}, s32[]{:S(2)}) async-start(s8[16777216]{0:T(1024)(128)(4,1)} %bitcast.53), calls=%async_computation.5 | async-start | bytes 8388608
  668.8 21.3 %slice-start.3 = ((s8[16777216]{0:T(1024)(128)(4,1)}), s8[4194304]{0:T(1024)(128)(4,1)S(1)}, s32[]{:S(2)}) async-start(s8[16777216]{0:T(1024)(128)(4,1)} %bitcast.53), calls=%async_computation.6 | async-start | bytes 8388608
  702.9 17.3 %copy-start.1 = (f32[2,512,512]{2,1,0:T(8,128)S(1)}, f32[2,512,512]{2,1,0:T(8,128)}, u32[]{:S(2)}) copy-start(f32[2,512,512]{2,1,0:T(8,128)} %param.21) | copy-start | bytes 6291460
Sparse Core Ops, SparseCore 0:
  142.4 348.6 reduce-scatter.1
  505.6 74.2 all-gather.1
where the time goes:
time: 735 us; the launch traced here: 727 us
  waiting for transfers between devices  411 us (56%)
  local copies, waits for them, and re-layouts  151 us (21%)
  other arithmetic  82.7 us (11%)
  matrix products  68.1 us (9%)
  between operations  14.6 us (2%)
    reduce_scatter x1, waiting for transfers between devices, per_device(): lax.psum_scatter(local_grad, 'dp', scatter_dimension=0, tiled=True) / n_dev  348 us
    all_gather x1, waiting for transfers between devices, per_device(): lax.all_gather(new_mom.astype(jnp.bfloat16), 'dp', axis=0, tiled=True)  62.8 us
    dot_general x2, matrix products, grad_blocks(): jnp.einsum('tri,tcj->rcij', x_pad, dy_pad, preferred_element_type=jnp.flo...  47 us
    transpose x2, local copies, waits for them, and re-layouts, grad_blocks(): jnp.einsum('tri,tcj->rcij', x_pad, dy_pad, preferred_element_type=jnp.flo...  34.9 us
    unnamed x24, local copies, waits for them, and re-layouts  29.3 us
    reshape x2, local copies, waits for them, and re-layouts, grad_blocks(): jnp.pad(dy_rows, ((0, 0), (0, out_blocks * block_dim - n_out)))  29 us
    convert_element_type x1, local copies, waits for them, and re-layouts, apply_update(): dir_fc2.astype(jnp.float32) + WEIGHT_DECAY * w_fc2  27.7 us
    concatenate x1, other arithmetic, per_device(): jnp.concatenate([grad_blocks(x_in, dy_mid, block_dim), grad_blocks(x_mid,...  24.1 us
  transfers between devices with their start and end apart: 2, of which 2 were waited for; matrix products, arithmetic and copies ran while one was open for 2% of the time, Pallas kernels for 0%

commit v1 on v0

v1 whole, which is shorter than its diff:
```python
import functools

import jax
import jax.numpy as jnp
from jax import lax
from jax.experimental import pallas as pl
from jax.experimental.pallas import tpu as pltpu
from jax.sharding import PartitionSpec as P

STEP = 10
STAT_DECAY = 0.999
MOM_DECAY = 0.9
GRAFT_EPS = 1e-8
LEARN_RATE = 0.01
WEIGHT_DECAY = 1e-4
BIAS_CORR = 1.0 - STAT_DECAY ** STEP

MESH = pl.DeviceIdType.MESH
B = 512
B2 = 2 * B
CH = 32
HALF = B // 2
DEPTH = 4
RING = 8
N_DEV = 16
ORDER = (7, 3, 5, 6, 1, 2, 4, 0)
LANDING = (0, 1, 2, 4, 3, 5, 6, 7)
AXES = ((1, 2, 4), (2, 4, 1), (4, 1, 2))
RS_ROWS = (((0, 176), (176, 168), (344, 168)), ((0, 168), (168, 176), (344, 168)))
AG_ROWS = (((0, 176), (176, 176), (352, 160)), ((0, 160), (160, 176), (336, 176)))
F32 = jnp.float32
BF16 = jnp.bfloat16


def flip(dev, mask):
    out = dev
    for bit in (1, 2, 4):
        if mask & bit:
            width = 2 * bit
            out = out + width - 2 * width * lax.rem(lax.div(dev, width), 2)
    return out


def other_core(dev):
    return dev + 1 - 2 * lax.rem(dev, 2)


def frame_mask(p, m):
    return sum(AXES[p][i] for i in range(3) if m & (1 << i))


def split(v):
    hi = v.astype(BF16)
    return hi, (v - hi.astype(F32)).astype(BF16)


def dot(a, b, ca, cb):
    return lax.dot_general(a, b, (((ca,), (cb,)), ((), ())), preferred_element_type=F32)


def dot_tn(a, b):
    return dot(a, b, 0, 0)


def dot3(a_hi, a_lo, b_hi, b_lo, ca, cb):
    return dot(a_hi, b_hi, ca, cb) + (dot(a_hi, b_lo, ca, cb) + dot(a_lo, b_hi, ca, cb))


def span(t, size):
    return pl.ds(pl.multiple_of(t * size, size), size)


def sweep(fn, init=None):
    def step(t, carry):
        out = fn(span(t, CH), carry)
        return carry if out is None else out

    return lax.fori_loop(0, B // CH, step, jnp.int32(0) if init is None else init)


def bits_of(rel, table, t):
    for n, value in enumerate(table):
        if n:
            rel = jnp.where(t == n, value, rel)
    return rel


def move(dev, rel):
    out = lax.rem(dev, 2)
    for bit in (1, 2, 4):
        out = out + 2 * bit * lax.rem(lax.div(dev, 2 * bit) + lax.div(rel, bit), 2)
    return out


def body(x_in, dy_mid, x_mid, dy_out, w1, w2, st_l, st_r, rt_l, rt_r, gsq, mom,
         w1a, w1b, w2v, o_l, o_r, o_a, o_m, dirs,
         xbuf, ybuf, res, dstage, tbuf, v_l, v_r, v_a, v_m,
         op_sem, st_sem, so_sem, rt_sem, w_sem, own_sem, db_sem, d2d_s, d2d_r, rs_s, rs_r, ag_s, ag_r, dd_s, dd_r, do_s, do_r):
    me = lax.axis_index('dp')
    core = lax.rem(me, 2)
    mate = other_core(me)

    barrier = pltpu.get_barrier_semaphore()
    for nb in (mate, flip(me, 1), flip(me, 2), flip(me, 4)):
        pl.semaphore_signal(barrier, inc=1, device_id=(nb,), device_id_type=MESH)

    def op_start(q):
        h = lax.rem(q, DEPTH)
        side = lax.div(q, DEPTH)
        dest = move(me, bits_of(jnp.int32(ORDER[0]), ORDER, lax.div(side, 2)))
        kd = jnp.where(lax.rem(side, 2) == 0, other_core(dest), dest)
        rows = span(h, B)

        @pl.when(dest < N_DEV // 2)
        def _():
            pltpu.make_async_copy(x_in.at[rows, span(lax.div(kd, 4), B)], xbuf.at[h], op_sem.at[0, h]).start()
            pltpu.make_async_copy(dy_mid.at[rows, span(lax.rem(kd, 4), B2)], ybuf.at[h], op_sem.at[1, h]).start()

        @pl.when(dest >= N_DEV // 2)
        def _():
            pltpu.make_async_copy(x_mid.at[rows, span(kd - N_DEV // 2, B)], xbuf.at[h], op_sem.at[0, h]).start()
            pltpu.make_async_copy(dy_out.at[rows, :], ybuf.at[h], op_sem.at[1, h]).start()

    def op_wait(h):
        pltpu.make_async_copy(x_in.at[pl.ds(0, B), pl.ds(0, B)], xbuf.at[h], op_sem.at[0, h]).wait()
        pltpu.make_async_copy(dy_mid.at[pl.ds(0, B), pl.ds(0, B2)], ybuf.at[h], op_sem.at[1, h]).wait()

    for q in range(DEPTH - 1):
        op_start(jnp.int32(q))
    states = ((st_l, v_l), (st_r, v_r), (gsq, v_a), (mom, v_m))
    for n, (src, dst) in enumerate(states):
        pltpu.make_async_copy(src, dst, st_sem.at[n]).start()
    pl.semaphore_wait(barrier, 4)

    def acc_at(i, r0, rn, c0, cn):
        return (w1a, w1b)[i // 4].at[pl.ds(r0, rn), pl.ds((i % 4) * B2 + c0, cn)]

    def acc_of(rel, s, p):
        r0, rn = RS_ROWS[s][p]
        return acc_at(ORDER.index(rel), r0, rn, s * B, B)

    def got(s, p, j):
        r0, rn = RS_ROWS[s][p]
        return w2v.at[j, pl.ds(r0, rn), pl.ds(s * B, B)]

    def rs_rel(p, j):
        a1, a2, a3 = AXES[p]
        return (a2 | a3, a2, a3, 0, a3, 0, 0)[j]

    def rs_copy(s, p, j):
        axis = AXES[p][0 if j < 4 else (1 if j < 6 else 2)]
        return pltpu.make_async_remote_copy(
            src_ref=acc_of(rs_rel(p, j) | axis, s, p), dst_ref=got(s, p, j),
            send_sem=rs_s.at[s, p, j], recv_sem=rs_r.at[s, p, j],
            device_id=(flip(me, axis),), device_id_type=MESH)

    def rs_take(s, p, j):
        rs_copy(s, p, j).wait_recv()
        ref = acc_of(rs_rel(p, j), s, p)
        ref[...] += got(s, p, j)[...]

    def d2d_copy(i, s, half):
        return pltpu.make_async_remote_copy(
            src_ref=res.at[lax.rem(i, 2), :, pl.ds(s * B, B)], dst_ref=half.at[:, span(lax.rem(i, 4) * 2 + s, B)],
            send_sem=d2d_s.at[s, i], recv_sem=d2d_r.at[s, i], device_id=(mate,), device_id_type=MESH)

    def on_half(i, fn):
        @pl.when(i < 4)
        def _():
            fn(w1a)

        @pl.when(i >= 4)
        def _():
            fn(w1b)

    def compute_step(i, _):
        @pl.when(i >= 2)
        def _():
            for s in range(2):
                d2d_copy(i - 2, s, w1a).wait_send()

        def side(j, _):
            out = jnp.where(j == 0, lax.rem(i, 2), 2)
            for h in range(DEPTH):
                ahead = (i * 2 + j) * DEPTH + h + DEPTH - 1

                @pl.when(ahead < 2 * 8 * DEPTH)
                def _(ahead=ahead):
                    op_start(ahead)
                op_wait(h)
                if h:
                    res[out] += dot_tn(xbuf[h], ybuf[h])
                else:
                    res[out] = dot_tn(xbuf[h], ybuf[h])

            @pl.when(j == 0)
            def _():
                on_half(i, lambda half: [d2d_copy(i, s, half).start() for s in range(2)])
            return 0

        lax.fori_loop(0, 2, side, 0)
        for s in range(2):
            def add_mine(half, s=s):
                d2d_copy(i, s, half).wait_recv()
                cols = span(lax.rem(i, 4) * 2 + s, B)

                def add_rows(rr, _):
                    half[rr, cols] += res[2, rr, pl.ds(s * B, B)]

                sweep(add_rows)

            on_half(i, add_mine)
            for ii in range(7):
                @pl.when(i == ii)
                def _(ii=ii, s=s):
                    for p in range(3):
                        for jj in range(4):
                            if (rs_rel(p, jj) | AXES[p][0]) == ORDER[ii]:
                                rs_copy(s, p, jj).start()
        return 0

    lax.fori_loop(0, 8, compute_step, 0)
    for s in range(2):
        for i in (6, 7):
            d2d_copy(i, s, w1b).wait_send()

    def root_half(s, side):
        return res.at[s, :, pl.ds(side * B, B)]

    for s in range(2):
        for side, src in enumerate((rt_l, rt_r)):
            pltpu.make_async_copy(src.at[s], root_half(s, side), rt_sem.at[s, side]).start()

    def root_hi(s, side):
        return ybuf.at[s, :, pl.ds(side * B, B)]

    def root_lo(s, side):
        return ybuf.at[2 + s, :, pl.ds(side * B, B)]

    def g_hi(s):
        return xbuf.at[s]

    def g_lo(s):
        return xbuf.at[2 + s]

    def prep_roots(s):
        for side, src in enumerate((rt_l, rt_r)):
            pltpu.make_async_copy(src.at[s], root_half(s, side), rt_sem.at[s, side]).wait()

        def rows(rr, _):
            for side in range(2):
                root_hi(s, side)[rr, :], root_lo(s, side)[rr, :] = split(root_half(s, side)[rr, :])

        sweep(rows)

    def state_wait(n):
        pltpu.make_async_copy(states[n][0], states[n][1], st_sem.at[n]).wait()

    def state_out(n):
        return pltpu.make_async_copy(states[n][1], (o_l, o_r, o_a, o_m)[n], so_sem.at[n])

    first_cols = pl.ds(0, B)

    def block_math(s):
        gref = acc_at(ORDER.index(0), 0, B, s * B, B)
        zero = jnp.zeros((8, B), F32)

        def first(rr, tot):
            g = gref[rr, :] * (1.0 / N_DEV)
            g_hi(s)[rr, :], g_lo(s)[rr, :] = split(g)
            sq = STAT_DECAY * v_a[s, rr, :] + (1.0 - STAT_DECAY) * g * g
            v_a[s, rr, :] = sq
            h = g / (jnp.sqrt(sq / BIAS_CORR) + GRAFT_EPS)
            return tot + jnp.sum((h * h).reshape(-1, 8, B), axis=0)

        h_sum = sweep(first, zero)

        def left(t, _):
            rr = span(t, HALF)
            v = dot3(root_hi(s, 0)[rr, :], root_lo(s, 0)[rr, :], g_hi(s)[...], g_lo(s)[...], 1, 0)
            tbuf[0, rr, :], tbuf[1, rr, :] = split(v)
            return 0

        lax.fori_loop(0, 2, left, 0)

        def right(t, tot):
            rr = span(t, HALF)
            v = dot3(tbuf[0, rr, :], tbuf[1, rr, :], root_hi(s, 1)[...], root_lo(s, 1)[...], 1, 0)
            res[2, rr, first_cols] = v
            return tot + jnp.sum((v * v).reshape(-1, 8, B), axis=0)

        p_sum = lax.fori_loop(0, 2, right, zero)
        ratio = jnp.sqrt(jnp.sum(h_sum, keepdims=True)) / jnp.sqrt(jnp.sum(p_sum, keepdims=True))

        def last(rr, _):
            m = MOM_DECAY * v_m[s, rr, :] + res[2, rr, first_cols] * ratio
            v_m[s, rr, :] = m
            dstage[s, rr, :] = m.astype(BF16)

        sweep(last)

    def stats(s):
        hi, lo = g_hi(s), g_lo(s)
        for t in range(2):
            rr = pl.ds(t * HALF, HALF)
            left = dot3(hi[rr, :], lo[rr, :], hi[...], lo[...], 1, 1)
            v_l[s, rr, :] = STAT_DECAY * v_l[s, rr, :] + (1.0 - STAT_DECAY) * left
            right = dot3(hi[:, rr], lo[:, rr], hi[...], lo[...], 0, 0)
            v_r[s, rr, :] = STAT_DECAY * v_r[s, rr, :] + (1.0 - STAT_DECAY) * right

    def rows_of(s, p, blk):
        r0, rn = AG_ROWS[s][p]
        return dirs.at[blk, pl.ds(r0, rn), :]

    def owner(p, m):
        return flip(me, frame_mask(p, m))

    def hi_bit(m):
        return 4 if m & 4 else (2 if m & 2 else 1)

    def ag_copy(s, p, m):
        top = hi_bit(m)
        held = m - top
        r0, rn = AG_ROWS[s][p]
        blk = 2 * owner(p, held) + s
        src = dstage.at[s, pl.ds(r0, rn), :] if held == 0 else rows_of(s, p, blk)
        return pltpu.make_async_remote_copy(
            src_ref=src, dst_ref=rows_of(s, p, blk), send_sem=ag_s.at[s, p, m - 1], recv_sem=ag_r.at[s, p, m - 1],
            device_id=(owner(p, top),), device_id_type=MESH)

    def ag_wait(s, p, m):
        ref = rows_of(s, p, 2 * owner(p, m) + s)
        pltpu.make_async_remote_copy(
            src_ref=ref, dst_ref=ref, send_sem=ag_s.at[s, p, m - 1], recv_sem=ag_r.at[s, p, m - 1],
            device_id=(mate,), device_id_type=MESH).wait_recv()

    def dd_copy(s, p, m):
        ref = rows_of(s, p, 2 * owner(p, m) + s)
        return pltpu.make_async_remote_copy(
            src_ref=ref, dst_ref=ref, send_sem=dd_s.at[s, p, m - 1], recv_sem=dd_r.at[s, p, m - 1],
            device_id=(mate,), device_id_type=MESH)

    def dd_wait(s, p, m):
        ref = rows_of(s, p, 2 * other_core(owner(p, m)) + s)
        pltpu.make_async_remote_copy(
            src_ref=ref, dst_ref=ref, send_sem=dd_s.at[s, p, m - 1], recv_sem=dd_r.at[s, p, m - 1],
            device_id=(mate,), device_id_type=MESH).wait_recv()

    def own_local(s):
        return pltpu.make_async_copy(dstage.at[s], dirs.at[2 * me + s], own_sem.at[s])

    def own_mate(s, recv=False):
        blk = 2 * (mate if recv else me) + s
        return pltpu.make_async_remote_copy(
            src_ref=dstage.at[s], dst_ref=dirs.at[blk], send_sem=do_s.at[s], recv_sem=do_r.at[s],
            device_id=(mate,), device_id_type=MESH)

    def ag_start(s):
        for m in (1, 2, 4):
            for p in range(3):
                ag_copy(s, p, m).start()
        own_mate(s).start()
        own_local(s).start()

    def ag_take(s, ms):
        for m in ms:
            for p in range(3):
                ag_wait(s, p, m)
                for nxt in (2, 4):
                    if nxt > m:
                        ag_copy(s, p, m | nxt).start()
                dd_copy(s, p, m).start()

    for j in range(4):
        for p in range(3):
            rs_take(0, p, j)
            if j < 2:
                rs_copy(0, p, 4 + j).start()
    prep_roots(0)
    prep_roots(1)
    for j in range(4):
        for p in range(3):
            rs_take(1, p, j)
    for p in range(3):
        rs_take(0, p, 4)
        rs_copy(0, p, 6).start()
    for j in range(2):
        for p in range(3):
            rs_copy(1, p, 4 + j).start()
    for j in (5, 6):
        for p in range(3):
            rs_take(0, p, j)
    for n in range(4):
        state_wait(n)
    block_math(0)
    ag_start(0)
    for p in range(3):
        rs_take(1, p, 4)
        rs_copy(1, p, 6).start()
    stats(0)
    for p in range(3):
        rs_take(1, p, 5)
    ag_take(0, (1, 2))
    for p in range(3):
        rs_take(1, p, 6)
    block_math(1)
    ag_start(1)

    for s in range(2):
        for p in range(3):
            for j in range(7):
                rs_copy(s, p, j).wait_send()

    def w_copies():
        out = []
        for n in range(4):
            rr = pl.ds(n * 128, 128)
            out.append(pltpu.make_async_copy(w1.at[rr, :], w1a.at[rr, :], w_sem.at[n]))
            out.append(pltpu.make_async_copy(w1.at[pl.ds(B + n * 128, 128), :], w1b.at[rr, :], w_sem.at[4 + n]))
        for n in range(8):
            out.append(pltpu.make_async_copy(w2.at[pl.ds(n * B, B), :], w2v.at[n], w_sem.at[8 + n]))
        return out

    for cp in w_copies():
        cp.start()
    for n in (2, 3):
        state_out(n).start()
    ag_take(0, (3,))
    stats(1)
    for n in range(2):
        state_out(n).start()

    def ring(slot):
        return ybuf.at[lax.div(slot, 2), :, span(lax.rem(slot, 2), B)]

    def d_load(blk, slot):
        return pltpu.make_async_copy(dirs.at[blk], ring(slot), db_sem.at[slot])

    def apply_rows(out_ref, c, slot):
        cols = span(c, B)

        def rows(rr, _):
            w = out_ref[rr, cols]
            out_ref[rr, cols] = w - LEARN_RATE * (ring(slot)[rr, :].astype(F32) + WEIGHT_DECAY * w)

        sweep(rows)

    def apply_block(blk, slot):
        @pl.when(blk < 8)
        def _():
            apply_rows(w1a, blk, slot)

        @pl.when((blk >= 8) & (blk < N_DEV))
        def _():
            apply_rows(w1b, blk - 8, slot)

        @pl.when(blk >= N_DEV)
        def _():
            apply_rows(w2v.at[lax.div(blk - N_DEV, 2)], lax.rem(blk, 2), slot)

    def apply_range(blk_of, first, last):
        def load(t):
            t = jnp.int32(t)
            return d_load(blk_of(t), lax.rem(t, RING))

        for t in range(first, min(first + RING, last)):
            load(t).start()

        def step(t, _):
            load(t).wait()
            apply_block(blk_of(t), lax.rem(t, RING))

            @pl.when(t + RING < last)
            def _():
                load(t + RING).start()
            return 0

        lax.fori_loop(first, last, step, 0)

    def arriving(dev):
        return lambda t: 2 * move(dev, bits_of(jnp.int32(LANDING[0]), LANDING, t)) + 1

    ag_take(1, (1, 2))
    ag_take(0, (4, 5, 6, 7))
    ag_take(1, (3,))
    for cp in w_copies():
        cp.wait()
    for s in range(2):
        own_local(s).wait()
    own_mate(0, True).wait_recv()
    for m in range(1, 8):
        for p in range(3):
            dd_wait(0, p, m)

    apply_range(lambda t: 2 * t, 0, N_DEV)
    own_mate(1, True).wait_recv()
    apply_range(arriving(me), 0, 1)
    apply_range(arriving(mate), 0, 1)
    for first, last, ms, ds in ((1, 4, (4,), (1, 2, 4)), (4, 7, (5, 6), (3, 5, 6)), (7, 8, (7,), (7,))):
        ag_take(1, ms)
        apply_range(arriving(me), first, last)
        for m in ds:
            for p in range(3):
                dd_wait(1, p, m)
        apply_range(arriving(mate), first, last)
    for n in range(4):
        state_out(n).wait()
    for s in range(2):
        own_mate(s).wait_send()
        for p in range(3):
            for m in range(1, 8):
                ag_copy(s, p, m).wait_send()
                dd_copy(s, p, m).wait_send()


def write_out(w1a, w1b, w2v, ow1, ow2, sem):
    pairs = [(w1a, ow1.at[pl.ds(0, B)]), (w1b, ow1.at[pl.ds(B, B)])]
    pairs += [(w2v.at[n], ow2.at[pl.ds(n * B, B)]) for n in range(8)]
    stores = [pltpu.make_async_copy(src, dst, sem.at[n]) for n, (src, dst) in enumerate(pairs)]
    for cp in stores:
        cp.start()
    for cp in stores:
        cp.wait()


def solution(mesh):
    def per_device(x_in, dy_mid, x_mid, dy_out, w_fc1, w_fc2, stat_left, stat_right, root_left, root_right, graft_sq, momentum):
        vmem = pl.BlockSpec(memory_space=pltpu.VMEM)
        hbm = pl.BlockSpec(memory_space=pltpu.HBM)
        dma = pltpu.SemaphoreType.DMA
        half = pltpu.VMEM((B, w_fc1.shape[1]), F32)
        state = pltpu.HBM(stat_left.shape, F32)
        held = pltpu.VMEM(stat_left.shape, F32)
        tiles = pltpu.VMEM((2, B, B), BF16)
        parts = dma((2, 3, 7))
        pair = dma((2,))
        w1a, w1b, w2v, *states, _ = pl.pallas_call(
            body,
            out_shape=(half, half, pltpu.VMEM((8, B, B2), F32), state, state, state, state, pltpu.HBM((2 * N_DEV, B, B), BF16)),
            in_specs=[hbm] * 12,
            out_specs=(vmem,) * 3 + (hbm,) * 5,
            scratch_shapes=[
                pltpu.VMEM((DEPTH, B, B), BF16), pltpu.VMEM((DEPTH, B, B2), BF16), pltpu.VMEM((3, B, B2), F32), tiles, tiles,
                held, held, held, held, dma((2, DEPTH)), dma((4,)), dma((4,)), dma((2, 2)), dma((16,)), pair, dma((RING,)), dma((2, 8)), dma((2, 8)),
                parts, parts, parts, parts, parts, parts, pair, pair],
            compiler_params=pltpu.CompilerParams(collective_id=0, has_side_effects=True, vmem_limit_bytes=24 << 20),
            name='shampoo_step',
        )(x_in, dy_mid, x_mid, dy_out, w_fc1, w_fc2, stat_left, stat_right, root_left, root_right, graft_sq, momentum)
        new_w1, new_w2 = pl.pallas_call(
            write_out,
            out_shape=(jax.ShapeDtypeStruct(w_fc1.shape, F32), jax.ShapeDtypeStruct(w_fc2.shape, F32)),
            in_specs=[vmem] * 3,
            out_specs=(hbm,) * 2,
            scratch_shapes=[dma((10,))],
            compiler_params=pltpu.CompilerParams(vmem_limit_bytes=1 << 20),
            name='write_out',
        )(w1a, w1b, w2v)
        return (new_w1, new_w2, *states)

    row_spec = P('dp', None)
    rep_spec = P(None, None)
    tile_spec = P('dp', None, None)
    in_specs = (row_spec, row_spec, row_spec, row_spec, rep_spec, rep_spec, tile_spec, tile_spec, tile_spec, tile_spec, tile_spec, tile_spec)
    out_specs = (rep_spec, rep_spec, tile_spec, tile_spec, tile_spec, tile_spec)
    return jax.shard_map(per_device, mesh=mesh, in_specs=in_specs, out_specs=out_specs, check_vma=False)
```

time: 735 us -> 208 us (0.28)
  waiting for transfers between devices: 411 us -> 0 us
  Pallas kernels: 0 us -> 199 us
  local copies, waits for them, and re-layouts: 151 us -> 8.36 us
  other arithmetic: 82.7 us -> 0 us
  matrix products: 68.1 us -> 0 us
  between operations: 14.6 us -> 0.68 us
    reduce_scatter x1 -> x0, waiting for transfers between devices: 348 us -> none  [per_device(): lax.psum_scatter(local_grad, 'dp', scatter_dimension=0, tiled=True) / n_dev]
    pallas_call x0 -> x2, Pallas kernels: none -> 199 us  [the longest x1 188 us: per_device(): pl.pallas_call(body, out_shape=(half, half, pltpu.VMEM((8, B, B2), F32),...]
    dot_general x6 -> x0, matrix products: 68.1 us -> none  [the longest x2 47 us: grad_blocks(): jnp.einsum('tri,tcj->rcij', x_pad, dy_pad, preferred_element_type=jnp.flo...]
    all_gather x1 -> x0, waiting for transfers between devices: 62.8 us -> none  [per_device(): lax.all_gather(new_mom.astype(jnp.bfloat16), 'dp', axis=0, tiled=True)]
    convert_element_type x2 -> x0, local copies, waits for them, and re-layouts: 45.9 us -> none  [the longest x1 27.7 us: apply_update(): dir_fc2.astype(jnp.float32) + WEIGHT_DECAY * w_fc2]
    transpose x2 -> x0, local copies, waits for them, and re-layouts: 34.9 us -> none  [grad_blocks(): jnp.einsum('tri,tcj->rcij', x_pad, dy_pad, preferred_element_type=jnp.flo...]
    sub x2 -> x0, other arithmetic: 30.1 us -> none  [the longest x1 17.3 us: apply_update(): w_fc1 - LEARN_RATE * (dir_fc1.astype(jnp.float32) + WEIGHT_DECAY * w_fc1)]
    reshape x2 -> x0, local copies, waits for them, and re-layouts: 29 us -> none  [grad_blocks(): jnp.pad(dy_rows, ((0, 0), (0, out_blocks * block_dim - n_out)))]
  transfers between devices with their start and end apart: 2 -> 0, of which waited for: 2 -> 0; matrix products, arithmetic and copies ran while one was open for 2% -> 0% of each run, Pallas kernels for 0% -> 0%
where the time goes in v1:
time: 208 us
  Pallas kernels  199 us (96%)
  local copies, waits for them, and re-layouts  8.36 us (4%)
    pallas_call x1, Pallas kernels, per_device(): pl.pallas_call(body, out_shape=(half, half, pltpu.VMEM((8, B, B2), F32),...  188 us
    pallas_call x1, Pallas kernels, per_device(): pl.pallas_call(write_out, out_shape=(jax.ShapeDtypeStruct(w_fc1.shape, F3...  11.2 us
    unnamed x12, local copies, waits for them, and re-layouts  8.36 us

profile of v1, /device:TPU:0, one launch (start us, length us, event | category | flops | bytes accessed | tf_op | source)
XLA Modules:
  0.0 207.8 jit_solution(11396678613264190496)
XLA Ops:
  0.6 187.5 %shampoo_step.1 = (f32[512,4096]{1,0:T(8,128)S(1)}, f32[512,4096]{1,0:T(8,128)S(1)}, f32[8,512,1024]{2,1,0:T(8,128)S(1)}, f32[2,512,512]{2,1,0:T(8,128)}, f32[2,...) custom-call(bf16[2048,1024]{1,0:T(8,128)(2,1)} %x_in.1, ...), custom_call_target="tpu_custom_call" | custom-call | tf_op jit(solution)/shard_map/shampoo_step/pallas_call | solution.py:537
  188.2 0.0 copy-start.3
  188.2 11.2 %write_out.1 = (f32[1024,4096]{1,0:T(8,128)}, f32[4096,1024]{1,0:T(8,128)}) custom-call(f32[512,4096]{1,0:T(8,128)S(1)} %get-tuple-element.15.w1a, f32[512,4096]{1,0:T(8,128)S(1)} %get-tuple-element.16.w1b, f32[8,512,1024]{2,1,0:T(8,128)S(1)} %get-tuple-element.17.w2v), custom_call_target="tpu_custom_call" | custom-call | tf_op jit(solution)/shard_map/write_out/pallas_call | solution.py:549
  199.4 0.0 copy-done.3
  199.4 0.0 copy-start.2
  199.4 1.3 copy.22
  200.7 1.0 copy-done.2
  201.7 0.0 copy-start.1
  201.7 1.3 copy.23
  203.1 1.0 copy-done.1
  204.1 0.0 copy-start
  204.1 1.3 copy.24
  205.4 1.0 copy-done
  206.4 1.3 copy.25
Async XLA Ops:
  188.2 11.2 %copy-start.3 = (f32[2,512,512]{2,1,0:T(8,128)S(1)}, f32[2,512,512]{2,1,0:T(8,128)}, u32[]{:S(2)}) copy-start(f32[2,512,512]{2,1,0:T(8,128)} %get-tuple-element.32) | copy-start | bytes 6291460
  199.4 2.3 %copy-start.2 = (f32[2,512,512]{2,1,0:T(8,128)S(1)}, f32[2,512,512]{2,1,0:T(8,128)}, u32[]{:S(2)}) copy-start(f32[2,512,512]{2,1,0:T(8,128)} %get-tuple-element.33) | copy-start | bytes 6291460
  201.7 2.3 %copy-start.1 = (f32[2,512,512]{2,1,0:T(8,128)S(1)}, f32[2,512,512]{2,1,0:T(8,128)}, u32[]{:S(2)}) copy-start(f32[2,512,512]{2,1,0:T(8,128)} %get-tuple-element.34) | copy-start | bytes 6291460
  204.1 2.3 %copy-start = (f32[2,512,512]{2,1,0:T(8,128)S(1)}, f32[2,512,512]{2,1,0:T(8,128)}, u32[]{:S(2)}) copy-start(f32[2,512,512]{2,1,0:T(8,128)} %get-tuple-element.35) | copy-start | bytes 6291460

commit v2 on v1

--- a/solution.py
+++ b/solution.py
@@ -22,6 +22,7 @@
 HALF = B // 2
 DEPTH = 4
 RING = 8
+VMEM_GRANT = 15 << 20
 N_DEV = 16
 ORDER = (7, 3, 5, 6, 1, 2, 4, 0)
 LANDING = (0, 1, 2, 4, 3, 5, 6, 7)
@@ -93,8 +94,8 @@
 
 
 def body(x_in, dy_mid, x_mid, dy_out, w1, w2, st_l, st_r, rt_l, rt_r, gsq, mom,
-         w1a, w1b, w2v, o_l, o_r, o_a, o_m, dirs,
-         xbuf, ybuf, res, dstage, tbuf, v_l, v_r, v_a, v_m,
+         w1a, w1b, w2v, v_l, v_r, v_m, kept, dirs,
+         xbuf, ybuf, res, dstage, late, v_a,
          op_sem, st_sem, so_sem, rt_sem, w_sem, own_sem, db_sem, d2d_s, d2d_r, rs_s, rs_r, ag_s, ag_r, dd_s, dd_r, do_s, do_r):
     me = lax.axis_index('dp')
     core = lax.rem(me, 2)
@@ -130,8 +131,6 @@
     states = ((st_l, v_l), (st_r, v_r), (gsq, v_a), (mom, v_m))
     for n, (src, dst) in enumerate(states):
         pltpu.make_async_copy(src, dst, st_sem.at[n]).start()
-    pl.semaphore_wait(barrier, 4)
-
     def acc_at(i, r0, rn, c0, cn):
         return (w1a, w1b)[i // 4].at[pl.ds(r0, rn), pl.ds((i % 4) * B2 + c0, cn)]
 
@@ -161,7 +160,7 @@
 
     def d2d_copy(i, s, half):
         return pltpu.make_async_remote_copy(
-            src_ref=res.at[lax.rem(i, 2), :, pl.ds(s * B, B)], dst_ref=half.at[:, span(lax.rem(i, 4) * 2 + s, B)],
+            src_ref=res.at[0, :, pl.ds(s * B, B)], dst_ref=half.at[:, span(lax.rem(i, 4) * 2 + s, B)],
             send_sem=d2d_s.at[s, i], recv_sem=d2d_r.at[s, i], device_id=(mate,), device_id_type=MESH)
 
     def on_half(i, fn):
@@ -174,13 +173,12 @@
             fn(w1b)
 
     def compute_step(i, _):
-        @pl.when(i >= 2)
+        @pl.when(i >= 1)
         def _():
             for s in range(2):
-                d2d_copy(i - 2, s, w1a).wait_send()
+                d2d_copy(i - 1, s, w1a).wait_send()
 
         def side(j, _):
-            out = jnp.where(j == 0, lax.rem(i, 2), 2)
             for h in range(DEPTH):
                 ahead = (i * 2 + j) * DEPTH + h + DEPTH - 1
 
@@ -189,9 +187,13 @@
                     op_start(ahead)
                 op_wait(h)
                 if h:
-                    res[out] += dot_tn(xbuf[h], ybuf[h])
+                    res[j] += dot_tn(xbuf[h], ybuf[h])
                 else:
-                    res[out] = dot_tn(xbuf[h], ybuf[h])
+                    res[j] = dot_tn(xbuf[h], ybuf[h])
+
+            @pl.when((i == 0) & (j == 0))
+            def _():
+                pl.semaphore_wait(barrier, 4)
 
             @pl.when(j == 0)
             def _():
@@ -205,7 +207,7 @@
                 cols = span(lax.rem(i, 4) * 2 + s, B)
 
                 def add_rows(rr, _):
-                    half[rr, cols] += res[2, rr, pl.ds(s * B, B)]
+                    half[rr, cols] += res[1, rr, pl.ds(s * B, B)]
 
                 sweep(add_rows)
 
@@ -221,8 +223,7 @@
 
     lax.fori_loop(0, 8, compute_step, 0)
     for s in range(2):
-        for i in (6, 7):
-            d2d_copy(i, s, w1b).wait_send()
+        d2d_copy(7, s, w1b).wait_send()
 
     def root_half(s, side):
         return res.at[s, :, pl.ds(side * B, B)]
@@ -256,8 +257,8 @@
     def state_wait(n):
         pltpu.make_async_copy(states[n][0], states[n][1], st_sem.at[n]).wait()
 
-    def state_out(n):
-        return pltpu.make_async_copy(states[n][1], (o_l, o_r, o_a, o_m)[n], so_sem.at[n])
+    def square_out():
+        return pltpu.make_async_copy(v_a, kept.at[0], so_sem.at[0])
 
     first_cols = pl.ds(0, B)
 
@@ -278,22 +279,22 @@
         def left(t, _):
             rr = span(t, HALF)
             v = dot3(root_hi(s, 0)[rr, :], root_lo(s, 0)[rr, :], g_hi(s)[...], g_lo(s)[...], 1, 0)
-            tbuf[0, rr, :], tbuf[1, rr, :] = split(v)
+            g_hi(1 - s)[rr, :], g_lo(1 - s)[rr, :] = split(v)
             return 0
 
         lax.fori_loop(0, 2, left, 0)
 
         def right(t, tot):
             rr = span(t, HALF)
-            v = dot3(tbuf[0, rr, :], tbuf[1, rr, :], root_hi(s, 1)[...], root_lo(s, 1)[...], 1, 0)
-            res[2, rr, first_cols] = v
+            v = dot3(g_hi(1 - s)[rr, :], g_lo(1 - s)[rr, :], root_hi(s, 1)[...], root_lo(s, 1)[...], 1, 0)
+            res[0, rr, first_cols] = v
             return tot + jnp.sum((v * v).reshape(-1, 8, B), axis=0)
 
         p_sum = lax.fori_loop(0, 2, right, zero)
         ratio = jnp.sqrt(jnp.sum(h_sum, keepdims=True)) / jnp.sqrt(jnp.sum(p_sum, keepdims=True))
 
         def last(rr, _):
-            m = MOM_DECAY * v_m[s, rr, :] + res[2, rr, first_cols] * ratio
+            m = MOM_DECAY * v_m[s, rr, :] + res[0, rr, first_cols] * ratio
             v_m[s, rr, :] = m
             dstage[s, rr, :] = m.astype(BF16)
 
@@ -318,33 +319,44 @@
     def hi_bit(m):
         return 4 if m & 4 else (2 if m & 2 else 1)
 
+    def landing(s, p, m, core_of=0):
+        if s == 1 and m == 7:
+            r0, rn = AG_ROWS[s][p]
+            return late.at[core_of, pl.ds(r0, rn), :]
+        dev = owner(p, m)
+        return rows_of(s, p, 2 * (other_core(dev) if core_of else dev) + s)
+
     def ag_copy(s, p, m):
         top = hi_bit(m)
         held = m - top
         r0, rn = AG_ROWS[s][p]
         blk = 2 * owner(p, held) + s
         src = dstage.at[s, pl.ds(r0, rn), :] if held == 0 else rows_of(s, p, blk)
+        dst = landing(s, p, m) if m == 7 and s == 1 else rows_of(s, p, blk)
         return pltpu.make_async_remote_copy(
-            src_ref=src, dst_ref=rows_of(s, p, blk), send_sem=ag_s.at[s, p, m - 1], recv_sem=ag_r.at[s, p, m - 1],
+            src_ref=src, dst_ref=dst, send_sem=ag_s.at[s, p, m - 1], recv_sem=ag_r.at[s, p, m - 1],
             device_id=(owner(p, top),), device_id_type=MESH)
 
     def ag_wait(s, p, m):
-        ref = rows_of(s, p, 2 * owner(p, m) + s)
+        ref = landing(s, p, m)
         pltpu.make_async_remote_copy(
             src_ref=ref, dst_ref=ref, send_sem=ag_s.at[s, p, m - 1], recv_sem=ag_r.at[s, p, m - 1],
             device_id=(mate,), device_id_type=MESH).wait_recv()
 
     def dd_copy(s, p, m):
-        ref = rows_of(s, p, 2 * owner(p, m) + s)
+        ref = landing(s, p, m)
         return pltpu.make_async_remote_copy(
-            src_ref=ref, dst_ref=ref, send_sem=dd_s.at[s, p, m - 1], recv_sem=dd_r.at[s, p, m - 1],
+            src_ref=ref, dst_ref=landing(s, p, m, 1) if m == 7 and s == 1 else ref,
+            send_sem=dd_s.at[s, p, m - 1], recv_sem=dd_r.at[s, p, m - 1],
             device_id=(mate,), device_id_type=MESH)
 
-    def dd_wait(s, p, m):
-        ref = rows_of(s, p, 2 * other_core(owner(p, m)) + s)
-        pltpu.make_async_remote_copy(
-            src_ref=ref, dst_ref=ref, send_sem=dd_s.at[s, p, m - 1], recv_sem=dd_r.at[s, p, m - 1],
-            device_id=(mate,), device_id_type=MESH).wait_recv()
+    def dd_wait(s, ms):
+        for m in ms:
+            for p in range(3):
+                ref = landing(s, p, m, 1)
+                pltpu.make_async_remote_copy(
+                    src_ref=ref, dst_ref=ref, send_sem=dd_s.at[s, p, m - 1], recv_sem=dd_r.at[s, p, m - 1],
+                    device_id=(mate,), device_id_type=MESH).wait_recv()
 
     def own_local(s):
         return pltpu.make_async_copy(dstage.at[s], dirs.at[2 * me + s], own_sem.at[s])
@@ -423,12 +435,9 @@
 
     for cp in w_copies():
         cp.start()
-    for n in (2, 3):
-        state_out(n).start()
+    square_out().start()
     ag_take(0, (3,))
     stats(1)
-    for n in range(2):
-        state_out(n).start()
 
     def ring(slot):
         return ybuf.at[lax.div(slot, 2), :, span(lax.rem(slot, 2), B)]
@@ -436,27 +445,27 @@
     def d_load(blk, slot):
         return pltpu.make_async_copy(dirs.at[blk], ring(slot), db_sem.at[slot])
 
-    def apply_rows(out_ref, c, slot):
+    def apply_rows(out_ref, c, src):
         cols = span(c, B)
 
         def rows(rr, _):
             w = out_ref[rr, cols]
-            out_ref[rr, cols] = w - LEARN_RATE * (ring(slot)[rr, :].astype(F32) + WEIGHT_DECAY * w)
+            out_ref[rr, cols] = w - LEARN_RATE * (src[rr, :].astype(F32) + WEIGHT_DECAY * w)
 
         sweep(rows)
 
-    def apply_block(blk, slot):
+    def apply_block(blk, src):
         @pl.when(blk < 8)
         def _():
-            apply_rows(w1a, blk, slot)
+            apply_rows(w1a, blk, src)
 
         @pl.when((blk >= 8) & (blk < N_DEV))
         def _():
-            apply_rows(w1b, blk - 8, slot)
+            apply_rows(w1b, blk - 8, src)
 
         @pl.when(blk >= N_DEV)
         def _():
-            apply_rows(w2v.at[lax.div(blk - N_DEV, 2)], lax.rem(blk, 2), slot)
+            apply_rows(w2v.at[lax.div(blk - N_DEV, 2)], lax.rem(blk, 2), src)
 
     def apply_range(blk_of, first, last):
         def load(t):
@@ -468,7 +477,7 @@
 
         def step(t, _):
             load(t).wait()
-            apply_block(blk_of(t), lax.rem(t, RING))
+            apply_block(blk_of(t), ring(lax.rem(t, RING)))
 
             @pl.when(t + RING < last)
             def _():
@@ -477,47 +486,60 @@
 
         lax.fori_loop(first, last, step, 0)
 
-    def arriving(dev):
-        return lambda t: 2 * move(dev, bits_of(jnp.int32(LANDING[0]), LANDING, t)) + 1
+    def arriving(dev, s):
+        return lambda t: 2 * move(dev, bits_of(jnp.int32(LANDING[0]), LANDING, t)) + s
+
+    def sent(s, ms):
+        for p in range(3):
+            for m in ms:
+                ag_copy(s, p, m).wait_send()
+                dd_copy(s, p, m).wait_send()
 
     ag_take(1, (1, 2))
-    ag_take(0, (4, 5, 6, 7))
-    ag_take(1, (3,))
     for cp in w_copies():
         cp.wait()
     for s in range(2):
         own_local(s).wait()
-    own_mate(0, True).wait_recv()
-    for m in range(1, 8):
-        for p in range(3):
-            dd_wait(0, p, m)
-
-    apply_range(lambda t: 2 * t, 0, N_DEV)
-    own_mate(1, True).wait_recv()
-    apply_range(arriving(me), 0, 1)
-    apply_range(arriving(mate), 0, 1)
-    for first, last, ms, ds in ((1, 4, (4,), (1, 2, 4)), (4, 7, (5, 6), (3, 5, 6)), (7, 8, (7,), (7,))):
-        ag_take(1, ms)
-        apply_range(arriving(me), first, last)
-        for m in ds:
-            for p in range(3):
-                dd_wait(1, p, m)
-        apply_range(arriving(mate), first, last)
-    for n in range(4):
-        state_out(n).wait()
-    for s in range(2):
         own_mate(s).wait_send()
-        for p in range(3):
-            for m in range(1, 8):
-                ag_copy(s, p, m).wait_send()
-                dd_copy(s, p, m).wait_send()
-
-
-def write_out(w1a, w1b, w2v, ow1, ow2, sem):
-    pairs = [(w1a, ow1.at[pl.ds(0, B)]), (w1b, ow1.at[pl.ds(B, B)])]
+        own_mate(s, True).wait_recv()
+    ag_take(0, (4, 5, 6))
+    apply_range(arriving(me, 0), 0, 7)
+    dd_wait(0, range(1, 7))
+    apply_range(arriving(mate, 0), 0, 7)
+    ag_take(0, (7,))
+    apply_range(arriving(me, 0), 7, 8)
+    apply_range(arriving(me, 1), 0, 1)
+    ag_take(1, (3,))
+    sent(0, range(1, 8))
+    dd_wait(0, (7,))
+    apply_range(arriving(mate, 0), 7, 8)
+    apply_range(arriving(mate, 1), 0, 1)
+    ag_take(1, (4,))
+    apply_range(arriving(me, 1), 1, 4)
+    ag_take(1, (5, 6))
+    dd_wait(1, (1, 2, 4))
+    apply_range(arriving(mate, 1), 1, 4)
+    apply_range(arriving(me, 1), 4, 7)
+    dd_wait(1, (3, 5, 6))
+    apply_range(arriving(mate, 1), 4, 7)
+    sent(1, range(1, 7))
+    square_out().wait()
+    ag_take(1, (7,))
+    apply_block(arriving(me, 1)(7), late.at[0])
+    dd_wait(1, (7,))
+    apply_block(arriving(mate, 1)(7), late.at[1])
+    sent(1, (7,))
+
+
+def write_out(w1a, w1b, w2v, v_l, v_r, v_m, kept, ow1, ow2, o_l, o_r, o_a, o_m, v_a, in_sem, sem):
+    load = pltpu.make_async_copy(kept.at[0], v_a, in_sem.at[0])
+    pairs = [(v_a, o_a), (v_l, o_l), (v_r, o_r), (v_m, o_m), (w1a, ow1.at[pl.ds(0, B)]), (w1b, ow1.at[pl.ds(B, B)])]
     pairs += [(w2v.at[n], ow2.at[pl.ds(n * B, B)]) for n in range(8)]
     stores = [pltpu.make_async_copy(src, dst, sem.at[n]) for n, (src, dst) in enumerate(pairs)]
-    for cp in stores:
+    for cp in [load] + stores[1:]:
+        cp.start()
+    load.wait()
+    for cp in stores[:1]:
         cp.start()
     for cp in stores:
         cp.wait()
@@ -529,33 +551,33 @@
         hbm = pl.BlockSpec(memory_space=pltpu.HBM)
         dma = pltpu.SemaphoreType.DMA
         half = pltpu.VMEM((B, w_fc1.shape[1]), F32)
-        state = pltpu.HBM(stat_left.shape, F32)
-        held = pltpu.VMEM(stat_left.shape, F32)
+        kept = pltpu.HBM((N_DEV,) + stat_left.shape, F32)
+        state = held = pltpu.VMEM(stat_left.shape, F32)
         tiles = pltpu.VMEM((2, B, B), BF16)
         parts = dma((2, 3, 7))
         pair = dma((2,))
-        w1a, w1b, w2v, *states, _ = pl.pallas_call(
+        *done, _ = pl.pallas_call(
             body,
-            out_shape=(half, half, pltpu.VMEM((8, B, B2), F32), state, state, state, state, pltpu.HBM((2 * N_DEV, B, B), BF16)),
+            out_shape=(half, half, pltpu.VMEM((8, B, B2), F32), state, state, state, kept, pltpu.HBM((2 * N_DEV, B, B), BF16)),
             in_specs=[hbm] * 12,
-            out_specs=(vmem,) * 3 + (hbm,) * 5,
+            out_specs=(vmem,) * 6 + (hbm,) * 2,
             scratch_shapes=[
-                pltpu.VMEM((DEPTH, B, B), BF16), pltpu.VMEM((DEPTH, B, B2), BF16), pltpu.VMEM((3, B, B2), F32), tiles, tiles,
-                held, held, held, held, dma((2, DEPTH)), dma((4,)), dma((4,)), dma((2, 2)), dma((16,)), pair, dma((RING,)), dma((2, 8)), dma((2, 8)),
+                pltpu.VMEM((DEPTH, B, B), BF16), pltpu.VMEM((DEPTH, B, B2), BF16), pltpu.VMEM((2, B, B2), F32), tiles, tiles, held,
+                dma((2, DEPTH)), dma((4,)), dma((1,)), dma((2, 2)), dma((16,)), pair, dma((RING,)), dma((2, 8)), dma((2, 8)),
                 parts, parts, parts, parts, parts, parts, pair, pair],
-            compiler_params=pltpu.CompilerParams(collective_id=0, has_side_effects=True, vmem_limit_bytes=24 << 20),
+            compiler_params=pltpu.CompilerParams(collective_id=0, has_side_effects=True, vmem_limit_bytes=VMEM_GRANT),
             name='shampoo_step',
         )(x_in, dy_mid, x_mid, dy_out, w_fc1, w_fc2, stat_left, stat_right, root_left, root_right, graft_sq, momentum)
-        new_w1, new_w2 = pl.pallas_call(
+        like = (w_fc1, w_fc2, stat_left, stat_right, graft_sq, momentum)
+        return pl.pallas_call(
             write_out,
-            out_shape=(jax.ShapeDtypeStruct(w_fc1.shape, F32), jax.ShapeDtypeStruct(w_fc2.shape, F32)),
-            in_specs=[vmem] * 3,
-            out_specs=(hbm,) * 2,
-            scratch_shapes=[dma((10,))],
-            compiler_params=pltpu.CompilerParams(vmem_limit_bytes=1 << 20),
+            out_shape=tuple(jax.ShapeDtypeStruct(v.shape, F32) for v in like),
+            in_specs=[vmem] * 6 + [hbm],
+            out_specs=(hbm,) * 6,
+            scratch_shapes=[held, dma((1,)), dma((14,))],
+            compiler_params=pltpu.CompilerParams(vmem_limit_bytes=VMEM_GRANT),
             name='write_out',
-        )(w1a, w1b, w2v)
-        return (new_w1, new_w2, *states)
+        )(*done)
 
     row_spec = P('dp', None)
     rep_spec = P(None, None)

time: 208 us -> 194 us (0.933)
  local copies, waits for them, and re-layouts: 8.36 us -> 0 us
  Pallas kernels: 199 us -> 193 us
    unnamed x12 -> x0, local copies, waits for them, and re-layouts: 8.36 us -> none
    pallas_call x1, Pallas kernels: 188 us -> 179 us  [per_device(): pl.pallas_call(body, out_shape=(half, half, pltpu.VMEM((8, B, B2), F32),...]
    pallas_call x1, Pallas kernels: 11.2 us -> 13.7 us  [per_device(): pl.pallas_call(write_out, out_shape=tuple((jax.ShapeDtypeStruct(v.shape,...]
where the time goes in v2:
time: 194 us
  Pallas kernels  193 us (99%)
    pallas_call x1, Pallas kernels, per_device(): pl.pallas_call(body, out_shape=(half, half, pltpu.VMEM((8, B, B2), F32),...  179 us
    pallas_call x1, Pallas kernels, per_device(): pl.pallas_call(write_out, out_shape=tuple((jax.ShapeDtypeStruct(v.shape,...  13.7 us

profile of v2, /device:TPU:0, one launch (start us, length us, event | category | flops | bytes accessed | tf_op | source)
XLA Modules:
  0.0 193.7 jit_solution(10530277870677832793)
XLA Ops:
  0.6 179.4 %shampoo_step.1 = (f32[512,4096]{1,0:T(8,128)S(1)}, f32[512,4096]{1,0:T(8,128)S(1)}, f32[8,512,1024]{2,1,0:T(8,128)S(1)}, f32[2,512,512]{2,1,0:T(8,128)S(1)}, f3...) custom-call(bf16[2048,1024]{1,0:T(8,128)(2,1)} %x_in.1, ...), custom_call_target="tpu_custom_call" | custom-call | tf_op jit(solution)/shard_map/shampoo_step/pallas_call | solution.py:559
  180.1 13.7 %write_out.1 = (f32[1024,4096]{1,0:T(8,128)}, f32[4096,1024]{1,0:T(8,128)}, f32[2,512,512]{2,1,0:T(8,128)}, f32[2,512,512]{2,1,0:T(8,128)}, f32[2,512,512]{2,1,0:T(8,128)}, /*index=5*/f32[2,512,512]{2,1,0:T(8,128)}) custom-call(f32[512,4096]{1,0:T(8,128)S(1)} %get-tuple-element.13.w1a, f32[512,4096]{1,0:T(8,128)S(1)} %get-tuple-element.14.w1b, ...), custom_call_target="tpu_custom_call" | custom-call | tf_op jit(solution)/shard_map/write_out/pallas_call | solution.py:572

commit v3 on v2

--- a/solution.py
+++ b/solution.py
@@ -129,8 +129,6 @@
     for q in range(DEPTH - 1):
         op_start(jnp.int32(q))
     states = ((st_l, v_l), (st_r, v_r), (gsq, v_a), (mom, v_m))
-    for n, (src, dst) in enumerate(states):
-        pltpu.make_async_copy(src, dst, st_sem.at[n]).start()
     def acc_at(i, r0, rn, c0, cn):
         return (w1a, w1b)[i // 4].at[pl.ds(r0, rn), pl.ds((i % 4) * B2 + c0, cn)]
 
@@ -150,18 +148,25 @@
         axis = AXES[p][0 if j < 4 else (1 if j < 6 else 2)]
         return pltpu.make_async_remote_copy(
             src_ref=acc_of(rs_rel(p, j) | axis, s, p), dst_ref=got(s, p, j),
-            send_sem=rs_s.at[s, p, j], recv_sem=rs_r.at[s, p, j],
+            send_sem=rs_s.at[0], recv_sem=rs_r.at[s, j],
             device_id=(flip(me, axis),), device_id_type=MESH)
 
-    def rs_take(s, p, j):
-        rs_copy(s, p, j).wait_recv()
-        ref = acc_of(rs_rel(p, j), s, p)
-        ref[...] += got(s, p, j)[...]
+    def wait_all(ref, send_sem, recv_sem):
+        return pltpu.make_async_remote_copy(
+            src_ref=ref, dst_ref=ref, send_sem=send_sem, recv_sem=recv_sem, device_id=(mate,), device_id_type=MESH)
+
+    def rs_take(s, j, then=()):
+        wait_all(w2v.at[j, :, pl.ds(s * B, B)], rs_s.at[0], rs_r.at[s, j]).wait_recv()
+        for p in range(3):
+            ref = acc_of(rs_rel(p, j), s, p)
+            ref[...] += got(s, p, j)[...]
+            for nxt in then:
+                rs_copy(s, p, nxt).start()
 
     def d2d_copy(i, s, half):
         return pltpu.make_async_remote_copy(
             src_ref=res.at[0, :, pl.ds(s * B, B)], dst_ref=half.at[:, span(lax.rem(i, 4) * 2 + s, B)],
-            send_sem=d2d_s.at[s, i], recv_sem=d2d_r.at[s, i], device_id=(mate,), device_id_type=MESH)
+            send_sem=d2d_s.at[0], recv_sem=d2d_r.at[s, lax.rem(i, 2)], device_id=(mate,), device_id_type=MESH)
 
     def on_half(i, fn):
         @pl.when(i < 4)
@@ -175,8 +180,7 @@
     def compute_step(i, _):
         @pl.when(i >= 1)
         def _():
-            for s in range(2):
-                d2d_copy(i - 1, s, w1a).wait_send()
+            wait_all(res.at[0], d2d_s.at[0], d2d_r.at[0, 0]).wait_send()
 
         def side(j, _):
             for h in range(DEPTH):
@@ -222,8 +226,10 @@
         return 0
 
     lax.fori_loop(0, 8, compute_step, 0)
-    for s in range(2):
-        d2d_copy(7, s, w1b).wait_send()
+    wait_all(res.at[0], d2d_s.at[0], d2d_r.at[0, 0]).wait_send()
+
+    for n, (src, dst) in enumerate(states):
+        pltpu.make_async_copy(src, dst, st_sem.at[n]).start()
 
     def root_half(s, side):
         return res.at[s, :, pl.ds(side * B, B)]
@@ -334,29 +340,21 @@
         src = dstage.at[s, pl.ds(r0, rn), :] if held == 0 else rows_of(s, p, blk)
         dst = landing(s, p, m) if m == 7 and s == 1 else rows_of(s, p, blk)
         return pltpu.make_async_remote_copy(
-            src_ref=src, dst_ref=dst, send_sem=ag_s.at[s, p, m - 1], recv_sem=ag_r.at[s, p, m - 1],
+            src_ref=src, dst_ref=dst, send_sem=ag_s.at[s], recv_sem=ag_r.at[s, m - 1],
             device_id=(owner(p, top),), device_id_type=MESH)
 
-    def ag_wait(s, p, m):
-        ref = landing(s, p, m)
-        pltpu.make_async_remote_copy(
-            src_ref=ref, dst_ref=ref, send_sem=ag_s.at[s, p, m - 1], recv_sem=ag_r.at[s, p, m - 1],
-            device_id=(mate,), device_id_type=MESH).wait_recv()
+    def tile_like(s, m, core_of):
+        return late.at[core_of] if m == 7 and s == 1 else dirs.at[0]
 
     def dd_copy(s, p, m):
         ref = landing(s, p, m)
         return pltpu.make_async_remote_copy(
             src_ref=ref, dst_ref=landing(s, p, m, 1) if m == 7 and s == 1 else ref,
-            send_sem=dd_s.at[s, p, m - 1], recv_sem=dd_r.at[s, p, m - 1],
-            device_id=(mate,), device_id_type=MESH)
+            send_sem=dd_s.at[s], recv_sem=dd_r.at[s, m - 1], device_id=(mate,), device_id_type=MESH)
 
     def dd_wait(s, ms):
         for m in ms:
-            for p in range(3):
-                ref = landing(s, p, m, 1)
-                pltpu.make_async_remote_copy(
-                    src_ref=ref, dst_ref=ref, send_sem=dd_s.at[s, p, m - 1], recv_sem=dd_r.at[s, p, m - 1],
-                    device_id=(mate,), device_id_type=MESH).wait_recv()
+            wait_all(tile_like(s, m, 1), dd_s.at[s], dd_r.at[s, m - 1]).wait_recv()
 
     def own_local(s):
         return pltpu.make_async_copy(dstage.at[s], dirs.at[2 * me + s], own_sem.at[s])
@@ -376,64 +374,44 @@
 
     def ag_take(s, ms):
         for m in ms:
+            wait_all(tile_like(s, m, 0), ag_s.at[s], ag_r.at[s, m - 1]).wait_recv()
+            for nxt in (2, 4):
+                if nxt > m:
+                    for p in range(3):
+                        ag_copy(s, p, m | nxt).start()
             for p in range(3):
-                ag_wait(s, p, m)
-                for nxt in (2, 4):
-                    if nxt > m:
-                        ag_copy(s, p, m | nxt).start()
                 dd_copy(s, p, m).start()
 
     for j in range(4):
-        for p in range(3):
-            rs_take(0, p, j)
-            if j < 2:
-                rs_copy(0, p, 4 + j).start()
+        rs_take(0, j, (4 + j,) if j < 2 else ())
     prep_roots(0)
     prep_roots(1)
     for j in range(4):
+        rs_take(1, j)
+    rs_take(0, 4, (6,))
+    for j in (4, 5):
         for p in range(3):
-            rs_take(1, p, j)
-    for p in range(3):
-        rs_take(0, p, 4)
-        rs_copy(0, p, 6).start()
-    for j in range(2):
-        for p in range(3):
-            rs_copy(1, p, 4 + j).start()
+            rs_copy(1, p, j).start()
     for j in (5, 6):
-        for p in range(3):
-            rs_take(0, p, j)
+        rs_take(0, j)
     for n in range(4):
         state_wait(n)
     block_math(0)
     ag_start(0)
-    for p in range(3):
-        rs_take(1, p, 4)
-        rs_copy(1, p, 6).start()
+    rs_take(1, 4, (6,))
     stats(0)
-    for p in range(3):
-        rs_take(1, p, 5)
+    rs_take(1, 5)
     ag_take(0, (1, 2))
-    for p in range(3):
-        rs_take(1, p, 6)
+    rs_take(1, 6)
     block_math(1)
     ag_start(1)
 
-    for s in range(2):
-        for p in range(3):
-            for j in range(7):
-                rs_copy(s, p, j).wait_send()
-
-    def w_copies():
-        out = []
-        for n in range(4):
-            rr = pl.ds(n * 128, 128)
-            out.append(pltpu.make_async_copy(w1.at[rr, :], w1a.at[rr, :], w_sem.at[n]))
-            out.append(pltpu.make_async_copy(w1.at[pl.ds(B + n * 128, 128), :], w1b.at[rr, :], w_sem.at[4 + n]))
-        for n in range(8):
-            out.append(pltpu.make_async_copy(w2.at[pl.ds(n * B, B), :], w2v.at[n], w_sem.at[8 + n]))
-        return out
-
-    for cp in w_copies():
+    wait_all(w2v.at[pl.ds(0, 7)], rs_s.at[0], rs_r.at[0, 0]).wait_send()
+    w_copies = [
+        pltpu.make_async_copy(w1.at[pl.ds(0, B)], w1a, w_sem.at[0]),
+        pltpu.make_async_copy(w1.at[pl.ds(B, B)], w1b, w_sem.at[1])]
+    w_copies += [pltpu.make_async_copy(w2.at[pl.ds(n * B, B)], w2v.at[n], w_sem.at[2 + n]) for n in range(8)]
+    for cp in w_copies:
         cp.start()
     square_out().start()
     ag_take(0, (3,))
@@ -467,68 +445,60 @@
         def _():
             apply_rows(w2v.at[lax.div(blk - N_DEV, 2)], lax.rem(blk, 2), src)
 
-    def apply_range(blk_of, first, last):
+    def apply_range(blk_of, last, early=None, ready=None):
         def load(t):
             t = jnp.int32(t)
-            return d_load(blk_of(t), lax.rem(t, RING))
-
-        for t in range(first, min(first + RING, last)):
+            return d_load(blk_of(t), t)
+
+        for t in range(last):
+            if t == early:
+                ready()
             load(t).start()
 
         def step(t, _):
             load(t).wait()
-            apply_block(blk_of(t), ring(lax.rem(t, RING)))
-
-            @pl.when(t + RING < last)
-            def _():
-                load(t + RING).start()
+            apply_block(blk_of(t), ring(t))
             return 0
 
-        lax.fori_loop(first, last, step, 0)
-
-    def arriving(dev, s):
-        return lambda t: 2 * move(dev, bits_of(jnp.int32(LANDING[0]), LANDING, t)) + s
-
-    def sent(s, ms):
-        for p in range(3):
-            for m in ms:
-                ag_copy(s, p, m).wait_send()
-                dd_copy(s, p, m).wait_send()
+        lax.fori_loop(0, last, step, 0)
+
+    def landed(dev, s, t):
+        return 2 * move(dev, bits_of(jnp.int32(LANDING[0]), LANDING, t)) + s
+
+    def between(dev):
+        return lambda t: landed(dev, jnp.where(t == 0, 0, 1), jnp.where(t == 0, 7, t - 1))
+
+    def sent(s):
+        wait_all(dirs.at[pl.ds(0, 7)], ag_s.at[s], ag_r.at[s, 0]).wait_send()
+        wait_all(dirs.at[pl.ds(0, 7)], dd_s.at[s], dd_r.at[s, 0]).wait_send()
 
     ag_take(1, (1, 2))
-    for cp in w_copies():
+    for cp in w_copies:
         cp.wait()
     for s in range(2):
         own_local(s).wait()
         own_mate(s).wait_send()
         own_mate(s, True).wait_recv()
     ag_take(0, (4, 5, 6))
-    apply_range(arriving(me, 0), 0, 7)
+    apply_range(lambda t: landed(me, 0, t), 7)
     dd_wait(0, range(1, 7))
-    apply_range(arriving(mate, 0), 0, 7)
+    apply_range(lambda t: landed(mate, 0, t), 7)
     ag_take(0, (7,))
-    apply_range(arriving(me, 0), 7, 8)
-    apply_range(arriving(me, 1), 0, 1)
+    ag_take(1, (4,))
+    apply_range(between(me), 5)
+    dd_wait(0, (7,))
+    dd_wait(1, (1, 2, 4))
+    apply_range(between(mate), 5)
     ag_take(1, (3,))
-    sent(0, range(1, 8))
-    dd_wait(0, (7,))
-    apply_range(arriving(mate, 0), 7, 8)
-    apply_range(arriving(mate, 1), 0, 1)
-    ag_take(1, (4,))
-    apply_range(arriving(me, 1), 1, 4)
+    sent(0)
+    square_out().wait()
     ag_take(1, (5, 6))
-    dd_wait(1, (1, 2, 4))
-    apply_range(arriving(mate, 1), 1, 4)
-    apply_range(arriving(me, 1), 4, 7)
-    dd_wait(1, (3, 5, 6))
-    apply_range(arriving(mate, 1), 4, 7)
-    sent(1, range(1, 7))
-    square_out().wait()
+    apply_range(lambda t: landed(jnp.where(t < 3, me, mate), 1, 4 + lax.rem(t, 3)), 6, 3, lambda: dd_wait(1, (3, 5, 6)))
     ag_take(1, (7,))
-    apply_block(arriving(me, 1)(7), late.at[0])
+    apply_block(landed(me, 1, 7), late.at[0])
     dd_wait(1, (7,))
-    apply_block(arriving(mate, 1)(7), late.at[1])
-    sent(1, (7,))
+    apply_block(landed(mate, 1, 7), late.at[1])
+    sent(1)
 
 
 def write_out(w1a, w1b, w2v, v_l, v_r, v_m, kept, ow1, ow2, o_l, o_r, o_a, o_m, v_a, in_sem, sem):
@@ -554,7 +524,7 @@
         kept = pltpu.HBM((N_DEV,) + stat_left.shape, F32)
         state = held = pltpu.VMEM(stat_left.shape, F32)
         tiles = pltpu.VMEM((2, B, B), BF16)
-        parts = dma((2, 3, 7))
+        parts = dma((2, 7))
         pair = dma((2,))
         *done, _ = pl.pallas_call(
             body,
@@ -563,8 +533,8 @@
             out_specs=(vmem,) * 6 + (hbm,) * 2,
             scratch_shapes=[
                 pltpu.VMEM((DEPTH, B, B), BF16), pltpu.VMEM((DEPTH, B, B2), BF16), pltpu.VMEM((2, B, B2), F32), tiles, tiles, held,
-                dma((2, DEPTH)), dma((4,)), dma((1,)), dma((2, 2)), dma((16,)), pair, dma((RING,)), dma((2, 8)), dma((2, 8)),
-                parts, parts, parts, parts, parts, parts, pair, pair],
+                dma((2, DEPTH)), dma((4,)), dma((1,)), dma((2, 2)), dma((10,)), pair, dma((RING,)), dma((1,)), dma((2, 2)),
+                dma((1,)), parts, pair, parts, pair, parts, pair, pair],
             compiler_params=pltpu.CompilerParams(collective_id=0, has_side_effects=True, vmem_limit_bytes=VMEM_GRANT),
             name='shampoo_step',
         )(x_in, dy_mid, x_mid, dy_out, w_fc1, w_fc2, stat_left, stat_right, root_left, root_right, graft_sq, momentum)

time: 194 us -> 187 us (0.964)
  Pallas kernels: 193 us -> 186 us
    pallas_call x1, Pallas kernels: 179 us -> 172 us  [per_device(): pl.pallas_call(body, out_shape=(half, half, pltpu.VMEM((8, B, B2), F32),...]
where the time goes in v3:
time: 187 us
  Pallas kernels  186 us (99%)
    pallas_call x1, Pallas kernels, per_device(): pl.pallas_call(body, out_shape=(half, half, pltpu.VMEM((8, B, B2), F32),...  172 us
    pallas_call x1, Pallas kernels, per_device(): pl.pallas_call(write_out, out_shape=tuple((jax.ShapeDtypeStruct(v.shape,...  13.7 us

profile of v3, /device:TPU:0, one launch (start us, length us, event | category | flops | bytes accessed | tf_op | source)
XLA Modules:
  0.0 186.5 jit_solution(7745389509889212919)
XLA Ops:
  0.6 172.2 %shampoo_step.1 = (f32[512,4096]{1,0:T(8,128)S(1)}, f32[512,4096]{1,0:T(8,128)S(1)}, f32[8,512,1024]{2,1,0:T(8,128)S(1)}, f32[2,512,512]{2,1,0:T(8,128)S(1)}, f3...) custom-call(bf16[2048,1024]{1,0:T(8,128)(2,1)} %x_in.1, ...), custom_call_target="tpu_custom_call" | custom-call | tf_op jit(solution)/shard_map/shampoo_step/pallas_call | solution.py:529
  172.9 13.7 %write_out.1 = (f32[1024,4096]{1,0:T(8,128)}, f32[4096,1024]{1,0:T(8,128)}, f32[2,512,512]{2,1,0:T(8,128)}, f32[2,512,512]{2,1,0:T(8,128)}, f32[2,512,512]{2,1,0:T(8,128)}, /*index=5*/f32[2,512,512]{2,1,0:T(8,128)}) custom-call(f32[512,4096]{1,0:T(8,128)S(1)} %get-tuple-element.13.w1a, f32[512,4096]{1,0:T(8,128)S(1)} %get-tuple-element.14.w1b, ...), custom_call_target="tpu_custom_call" | custom-call | tf_op jit(solution)/shard_map/write_out/pallas_call | solution.py:542

commit v4 on v3

--- a/solution.py
+++ b/solution.py
@@ -22,13 +22,13 @@
 HALF = B // 2
 DEPTH = 4
 RING = 8
-VMEM_GRANT = 15 << 20
+VMEM_GRANT = 27 << 19
 N_DEV = 16
 ORDER = (7, 3, 5, 6, 1, 2, 4, 0)
 LANDING = (0, 1, 2, 4, 3, 5, 6, 7)
 AXES = ((1, 2, 4), (2, 4, 1), (4, 1, 2))
 RS_ROWS = (((0, 176), (176, 168), (344, 168)), ((0, 168), (168, 176), (344, 168)))
-AG_ROWS = (((0, 176), (176, 176), (352, 160)), ((0, 160), (160, 176), (336, 176)))
+AG_ROWS = (((0, 176), (176, 176), (352, 160)), ((0, 176), (176, 160), (336, 176)))
 F32 = jnp.float32
 BF16 = jnp.bfloat16
 
@@ -94,9 +94,9 @@
 
 
 def body(x_in, dy_mid, x_mid, dy_out, w1, w2, st_l, st_r, rt_l, rt_r, gsq, mom,
-         w1a, w1b, w2v, v_l, v_r, v_m, kept, dirs,
-         xbuf, ybuf, res, dstage, late, v_a,
-         op_sem, st_sem, so_sem, rt_sem, w_sem, own_sem, db_sem, d2d_s, d2d_r, rs_s, rs_r, ag_s, ag_r, dd_s, dd_r, do_s, do_r):
+         w1a, w1b, w2v, v_l, v_r, v_a, v_m, dirs,
+         xbuf, ybuf, res, dstage, late,
+         op_sem, st_sem, rt_sem, w_sem, own_sem, db_sem, d2d_s, d2d_r, rs_s, rs_r, ag_s, ag_r, dd_s, dd_r, do_s, do_r):
     me = lax.axis_index('dp')
     core = lax.rem(me, 2)
     mate = other_core(me)
@@ -126,7 +126,7 @@
         pltpu.make_async_copy(x_in.at[pl.ds(0, B), pl.ds(0, B)], xbuf.at[h], op_sem.at[0, h]).wait()
         pltpu.make_async_copy(dy_mid.at[pl.ds(0, B), pl.ds(0, B2)], ybuf.at[h], op_sem.at[1, h]).wait()
 
-    for q in range(DEPTH - 1):
+    for q in range(DEPTH):
         op_start(jnp.int32(q))
     states = ((st_l, v_l), (st_r, v_r), (gsq, v_a), (mom, v_m))
     def acc_at(i, r0, rn, c0, cn):
@@ -177,10 +177,46 @@
         def _():
             fn(w1b)
 
+    def add_mine(i, s, half):
+        d2d_copy(i, s, half).wait_recv()
+        cols = span(lax.rem(i, 4) * 2 + s, B)
+
+        def add_rows(rr, _):
+            half[rr, cols] += res[1, rr, pl.ds(s * B, B)]
+
+        sweep(add_rows)
+
+    def send_on(ii, s):
+        for p in range(3):
+            for jj in range(4):
+                if (rs_rel(p, jj) | AXES[p][0]) == ORDER[ii]:
+                    rs_copy(s, p, jj).start()
+
+    for j in range(2):
+        for s in range(2):
+            cols = pl.ds(s * B, B)
+            for h in range(DEPTH):
+                if s == 0:
+                    op_wait(h)
+                    prod = dot_tn(xbuf[h], ybuf[h, :, cols])
+                else:
+                    prod = dot_tn(xbuf[h], ybuf[h, :, cols])
+                    if j == 0 or h < DEPTH - 1:
+                        op_start(jnp.int32((j + 1) * DEPTH + h))
+                if h:
+                    res[j, :, cols] += prod
+                else:
+                    res[j, :, cols] = prod
+            if j == 0:
+                if s == 0:
+                    pl.semaphore_wait(barrier, 4)
+                d2d_copy(jnp.int32(0), s, w1a).start()
+            else:
+                add_mine(jnp.int32(0), s, w1a)
+                send_on(0, s)
+
     def compute_step(i, _):
-        @pl.when(i >= 1)
-        def _():
-            wait_all(res.at[0], d2d_s.at[0], d2d_r.at[0, 0]).wait_send()
+        wait_all(res.at[0], d2d_s.at[0], d2d_r.at[0, 0]).wait_send()
 
         def side(j, _):
             for h in range(DEPTH):
@@ -195,10 +231,6 @@
                 else:
                     res[j] = dot_tn(xbuf[h], ybuf[h])
 
-            @pl.when((i == 0) & (j == 0))
-            def _():
-                pl.semaphore_wait(barrier, 4)
-
             @pl.when(j == 0)
             def _():
                 on_half(i, lambda half: [d2d_copy(i, s, half).start() for s in range(2)])
@@ -206,26 +238,14 @@
 
         lax.fori_loop(0, 2, side, 0)
         for s in range(2):
-            def add_mine(half, s=s):
-                d2d_copy(i, s, half).wait_recv()
-                cols = span(lax.rem(i, 4) * 2 + s, B)
-
-                def add_rows(rr, _):
-                    half[rr, cols] += res[1, rr, pl.ds(s * B, B)]
-
-                sweep(add_rows)
-
-            on_half(i, add_mine)
-            for ii in range(7):
+            on_half(i, lambda half, s=s: add_mine(i, s, half))
+            for ii in range(1, 7):
                 @pl.when(i == ii)
                 def _(ii=ii, s=s):
-                    for p in range(3):
-                        for jj in range(4):
-                            if (rs_rel(p, jj) | AXES[p][0]) == ORDER[ii]:
-                                rs_copy(s, p, jj).start()
+                    send_on(ii, s)
         return 0
 
-    lax.fori_loop(0, 8, compute_step, 0)
+    lax.fori_loop(1, 8, compute_step, 0)
     wait_all(res.at[0], d2d_s.at[0], d2d_r.at[0, 0]).wait_send()
 
     for n, (src, dst) in enumerate(states):
@@ -262,9 +282,6 @@
 
     def state_wait(n):
         pltpu.make_async_copy(states[n][0], states[n][1], st_sem.at[n]).wait()
-
-    def square_out():
-        return pltpu.make_async_copy(v_a, kept.at[0], so_sem.at[0])
 
     first_cols = pl.ds(0, B)
 
@@ -413,7 +430,6 @@
     w_copies += [pltpu.make_async_copy(w2.at[pl.ds(n * B, B)], w2v.at[n], w_sem.at[2 + n]) for n in range(8)]
     for cp in w_copies:
         cp.start()
-    square_out().start()
     ag_take(0, (3,))
     stats(1)
 
@@ -491,7 +507,6 @@
     apply_range(between(mate), 5)
     ag_take(1, (3,))
     sent(0)
-    square_out().wait()
     ag_take(1, (5, 6))
     apply_range(lambda t: landed(jnp.where(t < 3, me, mate), 1, 4 + lax.rem(t, 3)), 6, 3, lambda: dd_wait(1, (3, 5, 6)))
     ag_take(1, (7,))
@@ -501,15 +516,11 @@
     sent(1)
 
 
-def write_out(w1a, w1b, w2v, v_l, v_r, v_m, kept, ow1, ow2, o_l, o_r, o_a, o_m, v_a, in_sem, sem):
-    load = pltpu.make_async_copy(kept.at[0], v_a, in_sem.at[0])
-    pairs = [(v_a, o_a), (v_l, o_l), (v_r, o_r), (v_m, o_m), (w1a, ow1.at[pl.ds(0, B)]), (w1b, ow1.at[pl.ds(B, B)])]
+def write_out(w1a, w1b, w2v, v_l, v_r, v_a, v_m, ow1, ow2, o_l, o_r, o_a, o_m, sem):
+    pairs = [(w1a, ow1.at[pl.ds(0, B)]), (w1b, ow1.at[pl.ds(B, B)]), (v_l, o_l), (v_r, o_r), (v_a, o_a), (v_m, o_m)]
     pairs += [(w2v.at[n], ow2.at[pl.ds(n * B, B)]) for n in range(8)]
     stores = [pltpu.make_async_copy(src, dst, sem.at[n]) for n, (src, dst) in enumerate(pairs)]
-    for cp in [load] + stores[1:]:
-        cp.start()
-    load.wait()
-    for cp in stores[:1]:
+    for cp in stores:
         cp.start()
     for cp in stores:
         cp.wait()
@@ -521,19 +532,18 @@
         hbm = pl.BlockSpec(memory_space=pltpu.HBM)
         dma = pltpu.SemaphoreType.DMA
         half = pltpu.VMEM((B, w_fc1.shape[1]), F32)
-        kept = pltpu.HBM((N_DEV,) + stat_left.shape, F32)
-        state = held = pltpu.VMEM(stat_left.shape, F32)
+        state = pltpu.VMEM(stat_left.shape, F32)
         tiles = pltpu.VMEM((2, B, B), BF16)
         parts = dma((2, 7))
         pair = dma((2,))
         *done, _ = pl.pallas_call(
             body,
-            out_shape=(half, half, pltpu.VMEM((8, B, B2), F32), state, state, state, kept, pltpu.HBM((2 * N_DEV, B, B), BF16)),
+            out_shape=(half, half, pltpu.VMEM((8, B, B2), F32), state, state, state, state, pltpu.HBM((2 * N_DEV, B, B), BF16)),
             in_specs=[hbm] * 12,
-            out_specs=(vmem,) * 6 + (hbm,) * 2,
+            out_specs=(vmem,) * 7 + (hbm,),
             scratch_shapes=[
-                pltpu.VMEM((DEPTH, B, B), BF16), pltpu.VMEM((DEPTH, B, B2), BF16), pltpu.VMEM((2, B, B2), F32), tiles, tiles, held,
-                dma((2, DEPTH)), dma((4,)), dma((1,)), dma((2, 2)), dma((10,)), pair, dma((RING,)), dma((1,)), dma((2, 2)),
+                pltpu.VMEM((DEPTH, B, B), BF16), pltpu.VMEM((DEPTH, B, B2), BF16), pltpu.VMEM((2, B, B2), F32), tiles, tiles,
+                dma((2, DEPTH)), dma((4,)), dma((2, 2)), dma((10,)), pair, dma((RING,)), dma((1,)), dma((2, 2)),
                 dma((1,)), parts, pair, parts, pair, parts, pair, pair],
             compiler_params=pltpu.CompilerParams(collective_id=0, has_side_effects=True, vmem_limit_bytes=VMEM_GRANT),
             name='shampoo_step',
@@ -542,9 +552,9 @@
         return pl.pallas_call(
             write_out,
             out_shape=tuple(jax.ShapeDtypeStruct(v.shape, F32) for v in like),
-            in_specs=[vmem] * 6 + [hbm],
+            in_specs=[vmem] * 7,
             out_specs=(hbm,) * 6,
-            scratch_shapes=[held, dma((1,)), dma((14,))],
+            scratch_shapes=[dma((14,))],
             compiler_params=pltpu.CompilerParams(vmem_limit_bytes=VMEM_GRANT),
             name='write_out',
         )(*done)

time: 187 us -> 187 us (level)
  no operation moved by 1% of the time
where the time goes in v4:
time: 187 us; the launch traced here: 186 us
  Pallas kernels  186 us (99%)
    pallas_call x1, Pallas kernels, per_device(): pl.pallas_call(body, out_shape=(half, half, pltpu.VMEM((8, B, B2), F32),...  172 us
    pallas_call x1, Pallas kernels, per_device(): pl.pallas_call(write_out, out_shape=tuple((jax.ShapeDtypeStruct(v.shape,...  13.7 us

profile of v4, /device:TPU:0, one launch (start us, length us, event | category | flops | bytes accessed | tf_op | source)
XLA Modules:
  0.0 186.4 jit_solution(7109237797959885090)
XLA Ops:
  0.6 172.0 %shampoo_step.1 = (f32[512,4096]{1,0:T(8,128)S(1)}, f32[512,4096]{1,0:T(8,128)S(1)}, f32[8,512,1024]{2,1,0:T(8,128)S(1)}, f32[2,512,512]{2,1,0:T(8,128)S(1)}, f3...) custom-call(bf16[2048,1024]{1,0:T(8,128)(2,1)} %x_in.1, ...), custom_call_target="tpu_custom_call" | custom-call | tf_op jit(solution)/shard_map/shampoo_step/pallas_call | solution.py:539
  172.7 13.7 %write_out.1 = (f32[1024,4096]{1,0:T(8,128)}, f32[4096,1024]{1,0:T(8,128)}, f32[2,512,512]{2,1,0:T(8,128)}, f32[2,512,512]{2,1,0:T(8,128)}, f32[2,512,512]{2,1,0:T(8,128)}, /*index=5*/f32[2,512,512]{2,1,0:T(8,128)}) custom-call(f32[512,4096]{1,0:T(8,128)S(1)} %get-tuple-element.13.w1a, f32[512,4096]{1,0:T(8,128)S(1)} %get-tuple-element.14.w1b, ...), custom_call_target="tpu_custom_call" | custom-call | tf_op jit(solution)/shard_map/write_out/pallas_call | solution.py:552

commit v5 on v4

--- a/solution.py
+++ b/solution.py
@@ -126,8 +126,26 @@
         pltpu.make_async_copy(x_in.at[pl.ds(0, B), pl.ds(0, B)], xbuf.at[h], op_sem.at[0, h]).wait()
         pltpu.make_async_copy(dy_mid.at[pl.ds(0, B), pl.ds(0, B2)], ybuf.at[h], op_sem.at[1, h]).wait()
 
-    for q in range(DEPTH):
-        op_start(jnp.int32(q))
+    passes = ((0, 0), (1, 0), (0, 1), (1, 1))
+
+    def first_copies(n, h, fn):
+        j, s = passes[n]
+        kd = flip(me, ORDER[0]) if j else other_core(flip(me, ORDER[0]))
+        rows = pl.ds(h * B, B)
+        y_to = ybuf.at[h, :, pl.ds(0, B)]
+
+        @pl.when(kd < N_DEV // 2)
+        def _():
+            fn(pltpu.make_async_copy(x_in.at[rows, span(lax.div(kd, 4), B)], xbuf.at[h], op_sem.at[0, h]))
+            fn(pltpu.make_async_copy(dy_mid.at[rows, span(lax.rem(kd, 4) * 2 + s, B)], y_to, op_sem.at[1, h]))
+
+        @pl.when(kd >= N_DEV // 2)
+        def _():
+            fn(pltpu.make_async_copy(x_mid.at[rows, span(kd - N_DEV // 2, B)], xbuf.at[h], op_sem.at[0, h]))
+            fn(pltpu.make_async_copy(dy_out.at[rows, pl.ds(s * B, B)], y_to, op_sem.at[1, h]))
+
+    for h in range(DEPTH):
+        first_copies(0, h, lambda cp: cp.start())
     states = ((st_l, v_l), (st_r, v_r), (gsq, v_a), (mom, v_m))
     def acc_at(i, r0, rn, c0, cn):
         return (w1a, w1b)[i // 4].at[pl.ds(r0, rn), pl.ds((i % 4) * B2 + c0, cn)]
@@ -192,28 +210,26 @@
                 if (rs_rel(p, jj) | AXES[p][0]) == ORDER[ii]:
                     rs_copy(s, p, jj).start()
 
-    for j in range(2):
-        for s in range(2):
-            cols = pl.ds(s * B, B)
-            for h in range(DEPTH):
-                if s == 0:
-                    op_wait(h)
-                    prod = dot_tn(xbuf[h], ybuf[h, :, cols])
-                else:
-                    prod = dot_tn(xbuf[h], ybuf[h, :, cols])
-                    if j == 0 or h < DEPTH - 1:
-                        op_start(jnp.int32((j + 1) * DEPTH + h))
-                if h:
-                    res[j, :, cols] += prod
-                else:
-                    res[j, :, cols] = prod
-            if j == 0:
-                if s == 0:
-                    pl.semaphore_wait(barrier, 4)
-                d2d_copy(jnp.int32(0), s, w1a).start()
+    for n, (j, s) in enumerate(passes):
+        cols = pl.ds(s * B, B)
+        for h in range(DEPTH):
+            first_copies(n, h, lambda cp: cp.wait())
+            prod = dot_tn(xbuf[h], ybuf[h, :, pl.ds(0, B)])
+            if h:
+                res[j, :, cols] += prod
             else:
-                add_mine(jnp.int32(0), s, w1a)
-                send_on(0, s)
+                res[j, :, cols] = prod
+            if n + 1 < len(passes):
+                first_copies(n + 1, h, lambda cp: cp.start())
+            elif h < DEPTH - 1:
+                op_start(jnp.int32(2 * DEPTH + h))
+        if n == 0:
+            pl.semaphore_wait(barrier, 4)
+        if j == 0:
+            d2d_copy(jnp.int32(0), s, w1a).start()
+        if n >= 2:
+            add_mine(jnp.int32(0), n - 2, w1a)
+            send_on(0, n - 2)
 
     def compute_step(i, _):
         wait_all(res.at[0], d2d_s.at[0], d2d_r.at[0, 0]).wait_send()
@@ -517,7 +533,10 @@
 
 
 def write_out(w1a, w1b, w2v, v_l, v_r, v_a, v_m, ow1, ow2, o_l, o_r, o_a, o_m, sem):
-    pairs = [(w1a, ow1.at[pl.ds(0, B)]), (w1b, ow1.at[pl.ds(B, B)]), (v_l, o_l), (v_r, o_r), (v_a, o_a), (v_m, o_m)]
+    pairs = [(v_l, o_l), (v_r, o_r), (v_a, o_a), (v_m, o_m)]
+    for n in range(4):
+        rr = pl.ds(n * B // 4, B // 4)
+        pairs += [(w1a.at[rr], ow1.at[rr]), (w1b.at[rr], ow1.at[pl.ds(B + n * B // 4, B // 4)])]
     pairs += [(w2v.at[n], ow2.at[pl.ds(n * B, B)]) for n in range(8)]
     stores = [pltpu.make_async_copy(src, dst, sem.at[n]) for n, (src, dst) in enumerate(pairs)]
     for cp in stores:
@@ -554,7 +573,7 @@
             out_shape=tuple(jax.ShapeDtypeStruct(v.shape, F32) for v in like),
             in_specs=[vmem] * 7,
             out_specs=(hbm,) * 6,
-            scratch_shapes=[dma((14,))],
+            scratch_shapes=[dma((20,))],
             compiler_params=pltpu.CompilerParams(vmem_limit_bytes=VMEM_GRANT),
             name='write_out',
         )(*done)

time: 187 us -> 185 us (0.989)
  no operation moved by 1% of the time
where the time goes in v5:
time: 185 us
  Pallas kernels  185 us (100%)
    pallas_call x1, Pallas kernels, per_device(): pl.pallas_call(body, out_shape=(half, half, pltpu.VMEM((8, B, B2), F32),...  171 us
    pallas_call x1, Pallas kernels, per_device(): pl.pallas_call(write_out, out_shape=tuple((jax.ShapeDtypeStruct(v.shape,...  13.6 us

profile of v5, /device:TPU:0, one launch (start us, length us, event | category | flops | bytes accessed | tf_op | source)
XLA Modules:
  0.0 185.2 jit_solution(16034287640157383679)
XLA Ops:
  0.6 171.0 %shampoo_step.1 = (f32[512,4096]{1,0:T(8,128)S(1)}, f32[512,4096]{1,0:T(8,128)S(1)}, f32[8,512,1024]{2,1,0:T(8,128)S(1)}, f32[2,512,512]{2,1,0:T(8,128)S(1)}, f3...) custom-call(bf16[2048,1024]{1,0:T(8,128)(2,1)} %x_in.1, ...), custom_call_target="tpu_custom_call" | custom-call | tf_op jit(solution)/shard_map/shampoo_step/pallas_call | solution.py:558
  171.6 13.6 %write_out.1 = (f32[1024,4096]{1,0:T(8,128)}, f32[4096,1024]{1,0:T(8,128)}, f32[2,512,512]{2,1,0:T(8,128)}, f32[2,512,512]{2,1,0:T(8,128)}, f32[2,512,512]{2,1,0:T(8,128)}, /*index=5*/f32[2,512,512]{2,1,0:T(8,128)}) custom-call(f32[512,4096]{1,0:T(8,128)S(1)} %get-tuple-element.13.w1a, f32[512,4096]{1,0:T(8,128)S(1)} %get-tuple-element.14.w1b, ...), custom_call_target="tpu_custom_call" | custom-call | tf_op jit(solution)/shard_map/write_out/pallas_call | solution.py:571

commit v6 on v5

--- a/solution.py
+++ b/solution.py
@@ -22,7 +22,7 @@
 HALF = B // 2
 DEPTH = 4
 RING = 8
-VMEM_GRANT = 27 << 19
+VMEM_GRANT = 12 << 20
 N_DEV = 16
 ORDER = (7, 3, 5, 6, 1, 2, 4, 0)
 LANDING = (0, 1, 2, 4, 3, 5, 6, 7)
@@ -93,9 +93,32 @@
     return out
 
 
+def apply_to(w1a, w1b, w2v, blk, src):
+    def apply_rows(out_ref, c):
+        cols = span(c, B)
+
+        def rows(rr, _):
+            w = out_ref[rr, cols]
+            out_ref[rr, cols] = w - LEARN_RATE * (src[rr, :].astype(F32) + WEIGHT_DECAY * w)
+
+        sweep(rows)
+
+    @pl.when(blk < 8)
+    def _():
+        apply_rows(w1a, blk)
+
+    @pl.when((blk >= 8) & (blk < N_DEV))
+    def _():
+        apply_rows(w1b, blk - 8)
+
+    @pl.when(blk >= N_DEV)
+    def _():
+        apply_rows(w2v.at[lax.div(blk - N_DEV, 2)], lax.rem(blk, 2))
+
+
 def body(x_in, dy_mid, x_mid, dy_out, w1, w2, st_l, st_r, rt_l, rt_r, gsq, mom,
-         w1a, w1b, w2v, v_l, v_r, v_a, v_m, dirs,
-         xbuf, ybuf, res, dstage, late,
+         w1a, w1b, w2v, v_l, v_r, v_a, v_m, late, dirs,
+         xbuf, ybuf, res, dstage,
          op_sem, st_sem, rt_sem, w_sem, own_sem, db_sem, d2d_s, d2d_r, rs_s, rs_r, ag_s, ag_r, dd_s, dd_r, do_s, do_r):
     me = lax.axis_index('dp')
     core = lax.rem(me, 2)
@@ -455,27 +478,8 @@
     def d_load(blk, slot):
         return pltpu.make_async_copy(dirs.at[blk], ring(slot), db_sem.at[slot])
 
-    def apply_rows(out_ref, c, src):
-        cols = span(c, B)
-
-        def rows(rr, _):
-            w = out_ref[rr, cols]
-            out_ref[rr, cols] = w - LEARN_RATE * (src[rr, :].astype(F32) + WEIGHT_DECAY * w)
-
-        sweep(rows)
-
     def apply_block(blk, src):
-        @pl.when(blk < 8)
-        def _():
-            apply_rows(w1a, blk, src)
-
-        @pl.when((blk >= 8) & (blk < N_DEV))
-        def _():
-            apply_rows(w1b, blk - 8, src)
-
-        @pl.when(blk >= N_DEV)
-        def _():
-            apply_rows(w2v.at[lax.div(blk - N_DEV, 2)], lax.rem(blk, 2), src)
+        apply_to(w1a, w1b, w2v, blk, src)
 
     def apply_range(blk_of, last, early=None, ready=None):
         def load(t):
@@ -526,21 +530,36 @@
     ag_take(1, (5, 6))
     apply_range(lambda t: landed(jnp.where(t < 3, me, mate), 1, 4 + lax.rem(t, 3)), 6, 3, lambda: dd_wait(1, (3, 5, 6)))
     ag_take(1, (7,))
-    apply_block(landed(me, 1, 7), late.at[0])
     dd_wait(1, (7,))
-    apply_block(landed(mate, 1, 7), late.at[1])
     sent(1)
 
 
-def write_out(w1a, w1b, w2v, v_l, v_r, v_a, v_m, ow1, ow2, o_l, o_r, o_a, o_m, sem):
-    pairs = [(v_l, o_l), (v_r, o_r), (v_a, o_a), (v_m, o_m)]
-    for n in range(4):
-        rr = pl.ds(n * B // 4, B // 4)
-        pairs += [(w1a.at[rr], ow1.at[rr]), (w1b.at[rr], ow1.at[pl.ds(B + n * B // 4, B // 4)])]
-    pairs += [(w2v.at[n], ow2.at[pl.ds(n * B, B)]) for n in range(8)]
+def write_out(w1a, w1b, w2v, v_l, v_r, v_a, v_m, late, ow1, ow2, o_l, o_r, o_a, o_m, sem):
+    far = flip(lax.axis_index('dp'), 7)
+    first = 2 * far + 1
+    states = [(v_l, o_l), (v_r, o_r), (v_a, o_a), (v_m, o_m)]
+    spans = [pl.ds(n * B // 4, B // 4) for n in range(4)]
+    upper = [(w1a.at[rr], ow1.at[rr]) for rr in spans]
+    lower = [(w1b.at[rr], ow1.at[pl.ds(B + n * B // 4, B // 4)]) for n, rr in enumerate(spans)]
+    second = [(w2v.at[n], ow2.at[pl.ds(n * B, B)]) for n in range(8)]
+    pairs = states + upper + lower + second
     stores = [pltpu.make_async_copy(src, dst, sem.at[n]) for n, (src, dst) in enumerate(pairs)]
-    for cp in stores:
+
+    def go(lo, hi, when):
+        @pl.when(when)
+        def _():
+            for cp in stores[lo:hi]:
+                cp.start()
+
+    regions = ((4, 8, first < 8), (8, 12, (first >= 8) & (first < N_DEV)), (12, 20, first >= N_DEV))
+    for cp in stores[:4]:
         cp.start()
+    for lo, hi, held in regions:
+        go(lo, hi, jnp.logical_not(held))
+    apply_to(w1a, w1b, w2v, first, late.at[0])
+    apply_to(w1a, w1b, w2v, 2 * other_core(far) + 1, late.at[1])
+    for lo, hi, held in regions:
+        go(lo, hi, held)
     for cp in stores:
         cp.wait()
 
@@ -557,11 +576,11 @@
         pair = dma((2,))
         *done, _ = pl.pallas_call(
             body,
-            out_shape=(half, half, pltpu.VMEM((8, B, B2), F32), state, state, state, state, pltpu.HBM((2 * N_DEV, B, B), BF16)),
+            out_shape=(half, half, pltpu.VMEM((8, B, B2), F32), state, state, state, state, tiles, pltpu.HBM((2 * N_DEV, B, B), BF16)),
             in_specs=[hbm] * 12,
-            out_specs=(vmem,) * 7 + (hbm,),
+            out_specs=(vmem,) * 8 + (hbm,),
             scratch_shapes=[
-                pltpu.VMEM((DEPTH, B, B), BF16), pltpu.VMEM((DEPTH, B, B2), BF16), pltpu.VMEM((2, B, B2), F32), tiles, tiles,
+                pltpu.VMEM((DEPTH, B, B), BF16), pltpu.VMEM((DEPTH, B, B2), BF16), pltpu.VMEM((2, B, B2), F32), tiles,
                 dma((2, DEPTH)), dma((4,)), dma((2, 2)), dma((10,)), pair, dma((RING,)), dma((1,)), dma((2, 2)),
                 dma((1,)), parts, pair, parts, pair, parts, pair, pair],
             compiler_params=pltpu.CompilerParams(collective_id=0, has_side_effects=True, vmem_limit_bytes=VMEM_GRANT),
@@ -571,7 +590,7 @@
         return pl.pallas_call(
             write_out,
             out_shape=tuple(jax.ShapeDtypeStruct(v.shape, F32) for v in like),
-            in_specs=[vmem] * 7,
+            in_specs=[vmem] * 8,
             out_specs=(hbm,) * 6,
             scratch_shapes=[dma((20,))],
             compiler_params=pltpu.CompilerParams(vmem_limit_bytes=VMEM_GRANT),

time: 185 us -> 185 us (level)
  no operation moved by 1% of the time
where the time goes in v6:
time: 185 us
  Pallas kernels  184 us (99%)
    pallas_call x1, Pallas kernels, per_device(): pl.pallas_call(body, out_shape=(half, half, pltpu.VMEM((8, B, B2), F32),...  171 us
    pallas_call x1, Pallas kernels, per_device(): pl.pallas_call(write_out, out_shape=tuple((jax.ShapeDtypeStruct(v.shape,...  13.6 us

profile of v6, /device:TPU:0, one launch (start us, length us, event | category | flops | bytes accessed | tf_op | source)
XLA Modules:
  0.0 185.3 jit_solution(4133507872899082270)
XLA Ops:
  0.6 170.9 %shampoo_step.1 = (f32[512,4096]{1,0:T(8,128)S(1)}, f32[512,4096]{1,0:T(8,128)S(1)}, f32[8,512,1024]{2,1,0:T(8,128)S(1)}, f32[2,512,512]{2,1,0:T(8,128)S(1)}, f3...) custom-call(bf16[2048,1024]{1,0:T(8,128)(2,1)} %x_in.1, ...), custom_call_target="tpu_custom_call" | custom-call | tf_op jit(solution)/shard_map/shampoo_step/pallas_call | solution.py:577
  171.5 13.6 %write_out.1 = (f32[1024,4096]{1,0:T(8,128)}, f32[4096,1024]{1,0:T(8,128)}, f32[2,512,512]{2,1,0:T(8,128)}, f32[2,512,512]{2,1,0:T(8,128)}, f32[2,512,512]{2,1,0:T(8,128)}, /*index=5*/f32[2,512,512]{2,1,0:T(8,128)}) custom-call(f32[512,4096]{1,0:T(8,128)S(1)} %get-tuple-element.14.w1a, f32[512,4096]{1,0:T(8,128)S(1)} %get-tuple-element.15.w1b, ...), custom_call_target="tpu_custom_call" | custom-call | tf_op jit(solution)/shard_map/write_out/pallas_call | solution.py:590
